TPU v7x, 32 devices: a whole 2x2x4 slice. The times are simulated.
32 devices in a mesh: dp: 8 (over z, y), tensor: 4 (over x, core).
Axes of the slice: x: 2, y: 2, z: 4, core: 2. Of those that a mesh axis runs over, the one named last changes fastest.
Arguments:
- layer_in: bfloat16 [16384, 768], P('dp'), may hold values from -6 to 6
- block_of: int32 [16, 1024], P('dp'), may hold values from 0 to 7, never falling along the last dimension, each value on 1 to 256 neighbouring positions
- block_links: int32 [16, 8, 8], P('dp'), may hold values 0 or 1
- w_query: bfloat16 [768, 768], P(None, 'tensor'), may hold values from -0.21875 to 0.21875
- b_query: float32 [768], P('tensor'), may hold values from -1.5 to 1.5
- w_key: bfloat16 [768, 768], P(None, 'tensor'), may hold values from -0.21875 to 0.21875
- w_value: bfloat16 [768, 768], P(None, 'tensor'), may hold values from -0.21875 to 0.21875
- b_value: float32 [768], P('tensor'), may hold values from -1.5 to 1.5
- w_out: bfloat16 [768, 768], P('tensor'), may hold values from -1.75 to 1.75
- b_out: float32 [768], replicated, may hold values from -1.5 to 1.5
- gain_one: float32 [768], replicated, may hold values from 0.5 to 1.5
- shift_one: float32 [768], replicated, may hold values from -1.5 to 1.5
- w_up: bfloat16 [768, 3072], P(None, 'tensor'), may hold values from -0.21875 to 0.21875
- b_up: float32 [3072], P('tensor'), may hold values from -1.5 to 1.5
- w_down: bfloat16 [3072, 768], P('tensor'), may hold values from -0.109375 to 0.109375
- b_down: float32 [768], replicated, may hold values from -1.5 to 1.5
- gain_two: float32 [768], replicated, may hold values from 0.5 to 1.5
- shift_two: float32 [768], replicated, may hold values from -1.5 to 1.5
- grad_out: bfloat16 [16384, 768], P(('dp', 'tensor')), may hold values from -6 to 6
Outputs:
- layer_out: bfloat16 [16384, 768], P(('dp', 'tensor'))
- grad_in: float32 [16384, 768], P(('dp', 'tensor'))
- grad_w_query: float32 [768, 768], P('dp', 'tensor')
- grad_b_query: float32 [768], P('tensor')
- grad_w_key: float32 [768, 768], P('dp', 'tensor')
- grad_w_value: float32 [768, 768], P('dp', 'tensor')
- grad_b_value: float32 [768], P('tensor')
- grad_w_out: float32 [768, 768], P('tensor', 'dp')
- grad_b_out: float32 [768], replicated
- grad_gain_one: float32 [768], replicated
- grad_shift_one: float32 [768], replicated
- grad_w_up: float32 [768, 3072], P('dp', 'tensor')
- grad_b_up: float32 [3072], P('tensor')
- grad_w_down: float32 [3072, 768], P('tensor', 'dp')
- grad_b_down: float32 [768], replicated
- grad_gain_two: float32 [768], replicated
- grad_shift_two: float32 [768], replicated
Inputs may be any that keep to these rules, and one draw needn't show every extreme that they name: `block_of`: within a sequence the block numbers never fall and all 8 blocks occur; each block has 1 to 256 positions and one has exactly 256. `block_links`: only entries [sequence, i, j] with j < i are read.
All inputs are finite; a program needn't handle non-finite values. No bound on the sum of `block_links` on one device may be relied on, other than what follows from the above.
Results may differ from a plain program's by a relative error of at most 0.018.
Values may be sent and summed in bfloat16 or wider, within the bound.
No kernel may reach another device: no remote copies, remote signals or barrier semaphores. Data moves between devices by JAX's collectives and lax.ppermute only.
A program may use at most 128 MiB of HBM per device.

v0:
```python
import jax
import jax.numpy as jnp
from jax import lax
from jax.sharding import PartitionSpec as P

D = 768
HEADS = 12


EPS = 1e-06
NEG = -1e30
ROOT_HALF = 0.7071067811865476
INV_ROOT_TWO_PI = 0.3989422804014327


def matmul(left, right):
    return jnp.dot(left, right, preferred_element_type=jnp.float32)


def matmul_tn(left, right):
    return lax.dot_general(
        left, right, (((0,), (0,)), ((), ())), preferred_element_type=jnp.float32
    )


def matmul_nt(left, right):
    return lax.dot_general(
        left, right, (((1,), (1,)), ((), ())), preferred_element_type=jnp.float32
    )


def normalize(values):
    centre = values - jnp.mean(values, axis=-1, keepdims=True)
    inverse = lax.rsqrt(jnp.mean(centre * centre, axis=-1, keepdims=True) + EPS)
    return (centre * inverse, inverse)


def norm_back(upstream, normed, inverse, gain):
    shaped = upstream * gain
    centred = jnp.mean(shaped, axis=-1, keepdims=True)
    aligned = jnp.mean(shaped * normed, axis=-1, keepdims=True)
    return inverse * (shaped - centred - normed * aligned)


def gelu_slope(values):
    return 0.5 * (1.0 + lax.erf(values * ROOT_HALF)) + values * INV_ROOT_TWO_PI * jnp.exp(
        -0.5 * values * values
    )


def visible(query_blocks, key_blocks, link_table):
    count = link_table.shape[0]
    numbers = lax.iota(jnp.int32, count)
    same_block = numbers[:, None] == numbers[None, :]
    earlier = (numbers[:, None] > numbers[None, :]) & (link_table == 1)
    table = (same_block | earlier).astype(jnp.float32)
    query_onehot = (query_blocks[:, None] == numbers[None, :]).astype(jnp.float32)
    key_onehot = (key_blocks[:, None] == numbers[None, :]).astype(jnp.float32)
    return matmul_nt(matmul(query_onehot, table), key_onehot) > 0.5


def masked_scores(query_block, key_sequence, allowed, scale):
    raw = (
        jnp.einsum("qhd,khd->hqk", query_block, key_sequence, preferred_element_type=jnp.float32)
        * scale
    )
    return jnp.where(allowed[None], raw, NEG)


def split_heads(tensors, seqs, length):
    head_dim = D // HEADS
    return tuple(
        (tensor.reshape(seqs, length, tensor.shape[1] // head_dim, head_dim) for tensor in tensors)
    )


def attend_forward(query, key, value, block_of, block_links, scale, qblock):
    seqs, length = block_of.shape
    width = query.shape[1]
    query_heads, key_heads, value_heads = split_heads((query, key, value), seqs, length)

    def per_sequence(packed):
        query_seq, key_seq, value_seq, block_seq, link_seq = packed
        contexts = []
        totals = []
        for offset in range(0, length, qblock):
            query_block = query_seq[offset : offset + qblock]
            allowed = visible(block_seq[offset : offset + qblock], block_seq, link_seq)
            scores = masked_scores(query_block, key_seq, allowed, scale)
            highest = jnp.max(scores, axis=-1, keepdims=True)
            exponent = jnp.exp(scores - highest)
            summed = jnp.sum(exponent, axis=-1, keepdims=True)
            weights = (exponent / summed).astype(jnp.bfloat16)
            mixed = jnp.einsum(
                "hqk,khd->qhd", weights, value_seq, preferred_element_type=jnp.float32
            )
            contexts.append(mixed.reshape(qblock, width))
            totals.append((highest + jnp.log(summed))[:, :, 0])
        return (
            jnp.concatenate(contexts, axis=0).astype(jnp.bfloat16),
            jnp.concatenate(totals, axis=1),
        )

    context, log_totals = lax.map(
        per_sequence, (query_heads, key_heads, value_heads, block_of, block_links)
    )
    return (context.reshape(seqs * length, width), log_totals)


def attend_backward(
    query, key, value, grad_context, log_totals, block_of, block_links, scale, qblock
):
    seqs, length = block_of.shape
    width = query.shape[1]
    query_heads, key_heads, value_heads, grad_heads = split_heads(
        (query, key, value, grad_context), seqs, length
    )

    def per_sequence(packed):
        query_seq, key_seq, value_seq, grad_seq, total_seq, block_seq, link_seq = packed
        query_grads = []
        key_grad = jnp.zeros(key_seq.shape, jnp.float32)
        value_grad = jnp.zeros(value_seq.shape, jnp.float32)
        for offset in range(0, length, qblock):
            query_block = query_seq[offset : offset + qblock]
            grad_block = grad_seq[offset : offset + qblock]
            allowed = visible(block_seq[offset : offset + qblock], block_seq, link_seq)
            scores = masked_scores(query_block, key_seq, allowed, scale)
            probs = jnp.exp(scores - total_seq[:, offset : offset + qblock, None])
            pulled = jnp.einsum(
                "qhd,khd->hqk", grad_block, value_seq, preferred_element_type=jnp.float32
            )
            centre = jnp.sum(pulled * probs, axis=-1, keepdims=True)
            score_grad = (probs * (pulled - centre)).astype(jnp.bfloat16)
            block_query_grad = (
                jnp.einsum("hqk,khd->qhd", score_grad, key_seq, preferred_element_type=jnp.float32)
                * scale
            )
            query_grads.append(block_query_grad.reshape(qblock, width))
            key_grad = (
                key_grad
                + jnp.einsum(
                    "hqk,qhd->khd", score_grad, query_block, preferred_element_type=jnp.float32
                )
                * scale
            )
            value_grad = value_grad + jnp.einsum(
                "hqk,qhd->khd",
                probs.astype(jnp.bfloat16),
                grad_block,
                preferred_element_type=jnp.float32,
            )
        return (
            jnp.concatenate(query_grads, axis=0),
            key_grad.reshape(length, width),
            value_grad.reshape(length, width),
        )

    grad_query, grad_key, grad_value = lax.map(
        per_sequence,
        (query_heads, key_heads, value_heads, grad_heads, log_totals, block_of, block_links),
    )
    return (
        grad_query.reshape(seqs * length, width),
        grad_key.reshape(seqs * length, width),
        grad_value.reshape(seqs * length, width),
    )


def on_device(
    layer_in,
    block_of,
    block_links,
    w_query,
    b_query,
    w_key,
    w_value,
    b_value,
    w_out,
    b_out,
    gain_one,
    shift_one,
    w_up,
    b_up,
    w_down,
    b_down,
    gain_two,
    shift_two,
    grad_out,
):
    tokens, width = layer_in.shape
    ways = lax.axis_size("tensor")
    share = tokens // ways
    first_row = lax.axis_index("tensor") * share
    scale = float(D // HEADS) ** (-0.5)
    qblock = min(512, block_of.shape[1])
    query = (matmul(layer_in, w_query) + b_query).astype(jnp.bfloat16)
    key = matmul(layer_in, w_key).astype(jnp.bfloat16)
    value = (matmul(layer_in, w_value) + b_value).astype(jnp.bfloat16)
    context, log_totals = attend_forward(query, key, value, block_of, block_links, scale, qblock)
    branch = lax.psum(matmul(context, w_out), "tensor")
    normed_one, inverse_one = normalize(layer_in.astype(jnp.float32) + branch + b_out)
    hidden_one = normed_one * gain_one + shift_one
    hidden_low = hidden_one.astype(jnp.bfloat16)
    up = matmul(hidden_low, w_up) + b_up
    active = jax.nn.gelu(up, approximate=False).astype(jnp.bfloat16)
    ffn_mine = lax.psum_scatter(
        matmul(lax.slice_in_dim(active, 0, lax.axis_size("tensor") * share, axis=0), w_down),
        "tensor",
        scatter_dimension=0,
        tiled=True,
    )
    hidden_mine = lax.dynamic_slice_in_dim(hidden_one, first_row, share, 0)
    normed_two, inverse_two = normalize(hidden_mine + ffn_mine + b_down)
    layer_out = (normed_two * gain_two + shift_two).astype(jnp.bfloat16)
    upstream = grad_out.astype(jnp.float32)
    grad_gain_two = jnp.sum(upstream * normed_two, axis=0)
    grad_shift_two = jnp.sum(upstream, axis=0)
    grad_two = norm_back(upstream, normed_two, inverse_two, gain_two)
    grad_b_down = jnp.sum(grad_two, axis=0)
    ffn_grad = lax.all_gather(grad_two.astype(jnp.bfloat16), "tensor", axis=0, tiled=True)
    grad_w_down = matmul_tn(active, ffn_grad)
    grad_up = matmul_nt(ffn_grad, w_down) * gelu_slope(up)
    grad_b_up = jnp.sum(grad_up, axis=0)
    grad_up_low = grad_up.astype(jnp.bfloat16)
    grad_w_up = matmul_tn(hidden_low, grad_up_low)
    grad_hidden = grad_two + lax.psum_scatter(
        matmul_nt(lax.slice_in_dim(grad_up_low, 0, lax.axis_size("tensor") * share, axis=0), w_up),
        "tensor",
        scatter_dimension=0,
        tiled=True,
    )
    normed_mine = lax.dynamic_slice_in_dim(normed_one, first_row, share, 0)
    inverse_mine = lax.dynamic_slice_in_dim(inverse_one, first_row, share, 0)
    grad_gain_one = jnp.sum(grad_hidden * normed_mine, axis=0)
    grad_shift_one = jnp.sum(grad_hidden, axis=0)
    grad_one = norm_back(grad_hidden, normed_mine, inverse_mine, gain_one)
    grad_b_out = jnp.sum(grad_one, axis=0)
    branch_grad = lax.all_gather(grad_one.astype(jnp.bfloat16), "tensor", axis=0, tiled=True)
    grad_w_out = matmul_tn(context, branch_grad)
    grad_context = matmul_nt(branch_grad, w_out).astype(jnp.bfloat16)
    grad_query, grad_key, grad_value = attend_backward(
        query, key, value, grad_context, log_totals, block_of, block_links, scale, qblock
    )
    grad_b_query = jnp.sum(grad_query, axis=0)
    grad_b_value = jnp.sum(grad_value, axis=0)
    query_low = grad_query.astype(jnp.bfloat16)
    key_low = grad_key.astype(jnp.bfloat16)
    value_low = grad_value.astype(jnp.bfloat16)
    grad_w_query = matmul_tn(layer_in, query_low)
    grad_w_key = matmul_tn(layer_in, key_low)
    grad_w_value = matmul_tn(layer_in, value_low)
    part_query = lax.slice_in_dim(query_low, 0, lax.axis_size("tensor") * share, axis=0)
    grad_in = grad_one + lax.psum_scatter(
        (
            matmul_nt(part_query, w_query)
            + matmul_nt(key_low, w_key)
            + matmul_nt(value_low, w_value)
        ).astype(jnp.bfloat16),
        "tensor",
        scatter_dimension=0,
        tiled=True,
    ).astype(jnp.float32)
    input_side = (
        lax.psum_scatter(
            grad_w_query.astype(jnp.bfloat16), "dp", scatter_dimension=0, tiled=True
        ).astype(jnp.float32),
        lax.psum_scatter(
            grad_w_key.astype(jnp.bfloat16), "dp", scatter_dimension=0, tiled=True
        ).astype(jnp.float32),
        lax.psum_scatter(
            grad_w_value.astype(jnp.bfloat16), "dp", scatter_dimension=0, tiled=True
        ).astype(jnp.float32),
        lax.psum_scatter(
            grad_w_up.astype(jnp.bfloat16), "dp", scatter_dimension=0, tiled=True
        ).astype(jnp.float32),
    )
    output_side = (
        lax.psum_scatter(
            grad_w_out.astype(jnp.bfloat16), "dp", scatter_dimension=1, tiled=True
        ).astype(jnp.float32),
        lax.psum_scatter(
            grad_w_down.astype(jnp.bfloat16), "dp", scatter_dimension=1, tiled=True
        ).astype(jnp.float32),
    )
    column_sums = lax.psum((grad_b_query, grad_b_value, grad_b_up), "dp")
    row_sums = lax.psum(
        (grad_b_out, grad_gain_one, grad_shift_one, grad_b_down, grad_gain_two, grad_shift_two),
        ("dp", "tensor"),
    )
    return (
        layer_out,
        grad_in,
        input_side[0],
        column_sums[0],
        input_side[1],
        input_side[2],
        column_sums[1],
        output_side[0],
        row_sums[0],
        row_sums[1],
        row_sums[2],
        input_side[3],
        column_sums[2],
        output_side[1],
        row_sums[3],
        row_sums[4],
        row_sums[5],
    )


def solution(mesh):
    in_specs = (
        P("dp", None),
        P("dp", None),
        P("dp", None, None),
        P(None, "tensor"),
        P("tensor"),
        P(None, "tensor"),
        P(None, "tensor"),
        P("tensor"),
        P("tensor", None),
        P(),
        P(),
        P(),
        P(None, "tensor"),
        P("tensor"),
        P("tensor", None),
        P(),
        P(),
        P(),
        P(("dp", "tensor"), None),
    )
    out_specs = (
        P(("dp", "tensor"), None),
        P(("dp", "tensor"), None),
        P("dp", "tensor"),
        P("tensor"),
        P("dp", "tensor"),
        P("dp", "tensor"),
        P("tensor"),
        P("tensor", "dp"),
        P(),
        P(),
        P(),
        P("dp", "tensor"),
        P("tensor"),
        P("tensor", "dp"),
        P(),
        P(),
        P(),
    )
    return jax.shard_map(
        on_device, mesh=mesh, in_specs=in_specs, out_specs=out_specs, check_vma=False
    )
```

profile of v0, /device:TPU:0, one launch (start us, length us, event | category | flops | bytes accessed | tf_op | source)
XLA Modules:
  0.0 864.1 jit_solution(11577631656519245494)
XLA Ops:
  7.3 3.2 fusion.112
  11.3 3.1 fusion.111
  20.0 32.1 %while.26 = (s32[]{:T(128)}, bf16[2,1024,192]{1,2,0:T(8,128)(2,1)}, f32[2,3,1024]{2,1,0:T(4,128)}, bf16[2,1024,3,64]{1,3,2,0:T(8,128)(2,1)}, s32[2,1024]{1,0:T(2...) while((s32[]{:T(128)}, bf16[2,1024,192]{1,2,0:T(8,128)(2,1)}, ...), condition=%wide.region_5.6_spmd, body=%wide.region_0.5_spmd.sunk | while | flops 862019904 | bytes 56790224 | solution.py:104
  54.2 4.7 fusion.144
  59.0 122.4 %all-reduce.4.cloned.1.call-done = f32[2048,768]{1,0:T(8,128)} async-done(((f32[2048,768]{1,0:T(8,128)}), f32[2048,768]{1,0:T(8,128)}) %all-reduce.4.cloned.1.call-update) | async-done | bytes 6291472 | tf_op jit(solution)/shard_map/psum | solution.py:201
  181.4 4.7 fusion.116
  189.7 3.5 multiply_add_fusion
  193.2 17.1 %fusion.99 = (bf16[2048,768]{1,0:T(8,128)(2,1)S(1)}, f32[2048,768]{1,0:T(8,128)}) fusion(f32[768]{0:T(1024)S(1)} %copy-done.42, bf16[768,768]{1,0:T(8,128)(2,1)S(1)} %copy-done, f32[2048,768]{1,0:T(8,128)S(1)} %get-tuple-element.294), kind=kOutput, calls=%fused_computation.138 | convolution fusion | flops 2521300992 | bytes 16911360 | tf_op jit(solution)/shard_map/dot_general | solution.py:17
  212.0 4.4 fusion.145
  216.5 59.2 %reduce-scatter.18.cloned.1.call-done = f32[512,768]{1,0:T(8,128)} async-done(((f32[2048,768]{1,0:T(8,128)}), f32[512,768]{1,0:T(8,128)}) %reduce-scatter.18.cloned.1.call-update) | async-done | bytes 1572880 | tf_op jit(solution)/shard_map/reduce_scatter | solution.py:207
  283.8 28.6 %all-gather.3.cloned.1.call-done = bf16[2048,768]{1,0:T(8,128)(2,1)} async-done(((bf16[512,768]{1,0:T(8,128)(2,1)}), bf16[2048,768]{1,0:T(8,128)(2,1)}) %all-gather.3.cloned.1.call-update) | async-done | bytes 3145744 | tf_op jit(solution)/shard_map/all_gather | solution.py:221
  312.4 7.6 fusion.143
  321.7 4.5 fusion.123
  327.1 58.2 %reduce-scatter.20.cloned.1.call-done = f32[512,768]{1,0:T(8,128)} async-done(((f32[2048,768]{1,0:T(8,128)}), f32[512,768]{1,0:T(8,128)}) %reduce-scatter.20.cloned.1.call-update) | async-done | bytes 1572880 | tf_op jit(solution)/shard_map/reduce_scatter | solution.py:227
  385.3 3.6 multiply_reduce_fusion.3
  393.9 6.5 convolution_convert_fusion.2
  400.5 8.0 fusion.128
  408.6 13.4 %all-gather.5.cloned.1.call-done = bf16[2048,768]{1,0:T(8,128)(2,1)} async-done(((bf16[512,768]{1,0:T(8,128)(2,1)}), bf16[2048,768]{1,0:T(8,128)(2,1)}) %all-gather.5.cloned.1.call-update) | async-done | bytes 3145744 | tf_op jit(solution)/shard_map/all_gather | solution.py:239
  422.1 3.9 convolution_convert_fusion
  426.0 3.3 reshape.217
  435.3 46.6 %while.27 = (s32[]{:T(128)}, f32[2,1024,192]{1,2,0:T(8,128)}, bf16[2,1024,192]{1,2,0:T(8,128)(2,1)}, f32[2,1024,192]{1,2,0:T(8,128)}, bf16[2,1024,3,64]{1,3,2,0:...) while((s32[]{:T(128)}, f32[2,1024,192]{1,2,0:T(8,128)}, ...), condition=%wide.region_20.21_spmd, body=%wide.region_17.20_spmd.sunk | while | flops 2079610112 | bytes 146298720 | solution.py:159
  482.0 3.9 fusion.141
  491.6 3.7 fusion.147
  499.0 3.7 fusion.146
  502.9 7.6 add_convert_fusion
  512.2 45.3 %reduce-scatter.24.cloned.1.call-done = bf16[96,768]{1,0:T(8,128)(2,1)} async-done(((bf16[768,768]{1,0:T(8,128)(2,1)}), bf16[96,768]{1,0:T(8,128)(2,1)}) %reduce-scatter.24.cloned.1.call-update) | async-done | bytes 147472 | tf_op jit(solution)/shard_map/reduce_scatter | solution.py:274
  559.1 40.7 %all-reduce = (f32[768]{0:T(1024)}, f32[768]{0:T(1024)}, f32[768]{0:T(1024)}, f32[768]{0:T(1024)}, f32[768]{0:T(1024)}, /*index=5*/f32[768]{0:T(1024)}) all-reduce(f32[768]{0:T(1024)} %get-tuple-element.289, f32[768]{0:T(1024)S(1)} %copy-done.36, f32[768]{0:T(1024)S(1)} %copy-done.37, ...), channel_id=1, replica_groups=mesh['dp'=8,'tensor'=4] {'dp','tensor'}, use_global_device_ids=true, to_apply=%region_31.32 | all-reduce | flops 4608 | bytes 36864 | tf_op jit(solution)/shard_map/psum | solution.py:287
  599.9 21.9 %all-reduce.1 = (f32[192]{0:T(256)}, f32[192]{0:T(256)}, f32[768]{0:T(1024)}) all-reduce(f32[192]{0:T(256)} %get-tuple-element.324, f32[192]{0:T(256)} %get-tuple-element.315, f32[768]{0:T(1024)} %get-tuple-element.321), channel_id=1, replica_groups=mesh['dp'=8,'tensor'=4] {'dp'}, use_global_device_ids=true, to_apply=%region_24.25 | all-reduce | flops 1152 | bytes 9216 | tf_op jit(solution)/shard_map/psum | solution.py:286
  623.5 63.0 %reduce-scatter.32.cloned.1.call-done = bf16[96,192]{1,0:T(8,128)(2,1)} async-done(((bf16[768,192]{1,0:T(8,128)(2,1)}), bf16[96,192]{1,0:T(8,128)(2,1)}) %reduce-scatter.32.cloned.1.call-update) | async-done | bytes 36880
  688.2 62.6 %reduce-scatter.28.cloned.1.call-done = bf16[96,192]{1,0:T(8,128)(2,1)} async-done(((bf16[768,192]{1,0:T(8,128)(2,1)}), bf16[96,192]{1,0:T(8,128)(2,1)}) %reduce-scatter.28.cloned.1.call-update) | async-done | bytes 36880
  752.5 62.8 %reduce-scatter.30.cloned.1.call-done = bf16[96,192]{1,0:T(8,128)(2,1)} async-done(((bf16[768,192]{1,0:T(8,128)(2,1)}), bf16[96,192]{1,0:T(8,128)(2,1)}) %reduce-scatter.30.cloned.1.call-update) | async-done | bytes 36880
  817.0 37.7 %reduce-scatter.22.cloned.1.call-done = bf16[512,768]{1,0:T(8,128)(2,1)} async-done(((bf16[2048,768]{1,0:T(8,128)(2,1)}), bf16[512,768]{1,0:T(8,128)(2,1)}) %reduce-scatter.22.cloned.1.call-update) | async-done | bytes 786448 | tf_op jit(solution)/shard_map/reduce_scatter | solution.py:254
  (263 shorter events, 135.2 us)
Async XLA Ops:
  7.2 185.9 %copy-start = (bf16[768,768]{1,0:T(8,128)(2,1)S(1)}, bf16[768,768]{1,0:T(8,128)(2,1)}, u32[]{:S(2)}) copy-start(bf16[768,768]{1,0:T(8,128)(2,1)} %param.35) | copy-start | bytes 3538948
  7.2 174.2 %all-reduce.4.cloned.1.call-start = ((), (), s32[]{:S(2)}) async-start(), calls=%async_computation.9 | async-start | bytes 12582912 | tf_op jit(solution)/shard_map/psum | solution.py:201
  14.4 5.6 copy-start.20
  14.4 5.6 copy-start.29
  54.2 127.2 %copy-start.31 = (f32[768]{0:T(1024)S(1)}, f32[768]{0:T(1024)}, u32[]{:S(2)}) copy-start(f32[768]{0:T(1024)} %param.32) | copy-start | bytes 9220
  58.9 216.8 %reduce-scatter.18.cloned.1.call-start = ((), (), s32[]{:S(2)}) async-start(), calls=%async_computation.10 | async-start | bytes 7864320 | tf_op jit(solution)/shard_map/reduce_scatter | solution.py:207
  181.4 6.5 copy-start.4
  193.1 17.1 %copy-start.11 = (f32[2048,768]{1,0:T(8,128)}, f32[2048,768]{1,0:T(8,128)S(1)}, u32[]{:S(2)}) copy-start(f32[2048,768]{1,0:T(8,128)S(1)} %get-tuple-element.294) | copy-start | bytes 18874372
  193.1 18.8 %copy-start.41 = (bf16[768,768]{1,0:T(8,128)(2,1)S(1)}, bf16[768,768]{1,0:T(8,128)(2,1)}, u32[]{:S(2)}) copy-start(bf16[768,768]{1,0:T(8,128)(2,1)} %param.37) | copy-start | bytes 3538948
  216.4 61.8 %copy-start.15 = (bf16[512,768]{1,0:T(8,128)(2,1)S(1)}, bf16[512,768]{1,0:T(8,128)(2,1)}, u32[]{:S(2)}) copy-start(bf16[512,768]{1,0:T(8,128)(2,1)} %param.41) | copy-start | bytes 2359300
  216.4 96.0 %all-gather.3.cloned.1.call-start = ((), (), s32[]{:S(2)}) async-start(), calls=%async_computation.11 | async-start | bytes 3932160 | tf_op jit(solution)/shard_map/all_gather | solution.py:221
  283.8 101.5 %reduce-scatter.20.cloned.1.call-start = ((), (), s32[]{:S(2)}) async-start(), calls=%async_computation.12 | async-start | bytes 7864320 | tf_op jit(solution)/shard_map/reduce_scatter | solution.py:227
  326.2 59.0 %copy-start.33 = (f32[768]{0:T(1024)S(1)}, f32[768]{0:T(1024)}, u32[]{:S(2)}) copy-start(f32[768]{0:T(1024)} %param.33) | copy-start | bytes 9220
  326.3 95.8 %all-gather.5.cloned.1.call-start = ((), (), s32[]{:S(2)}) async-start(), calls=%async_computation.13 | async-start | bytes 3932160 | tf_op jit(solution)/shard_map/all_gather | solution.py:239
  393.4 117.1 %reduce-scatter.26.cloned.1.call-start = ((), (), s32[]{:S(2)}) async-start(), calls=%async_computation.16 | async-start | bytes 1327104 | tf_op jit(solution)/shard_map/reduce_scatter | solution.py:282
  400.4 21.7 %copy-start.26 = (bf16[192,768]{1,0:T(8,128)(2,1)S(1)}, bf16[192,768]{1,0:T(8,128)(2,1)}, u32[]{:S(2)}) copy-start(bf16[192,768]{1,0:T(8,128)(2,1)} %param.31) | copy-start | bytes 884740
  400.4 157.0 %reduce-scatter.24.cloned.1.call-start = ((), (), s32[]{:S(2)}) async-start(), calls=%async_computation.15 | async-start | bytes 1327104 | tf_op jit(solution)/shard_map/reduce_scatter | solution.py:274
  408.5 23.0 %copy-start.13 = (bf16[2,24,8,1024]{3,2,0,1:T(8,128)(2,1)S(1)}, bf16[2,24,8,1024]{3,2,0,1:T(8,128)(2,1)}, u32[]{:S(2)}) copy-start(bf16[2,24,8,1024]{3,2,0,1:T(8,128)(2,1)} %copy-done.12) | copy-start | bytes 2359300
  408.6 213.4 %reduce-scatter.34.cloned.1.call-start = ((), (), s32[]{:S(2)}) async-start(), calls=%async_computation.20 | async-start | bytes 442368
  408.6 26.7 %copy-start.7 = (bf16[2,1024,3,64]{1,3,2,0:T(8,128)(2,1)S(1)}, bf16[2,1024,3,64]{1,3,2,0:T(8,128)(2,1)}, u32[]{:S(2)}) copy-start(bf16[2,1024,3,64]{1,3,2,0:T(8,128)(2,1)} %get-tuple-element.571) | copy-start | bytes 2359300
  435.3 251.3 %reduce-scatter.32.cloned.1.call-start = ((), (), s32[]{:S(2)}) async-start(), calls=%async_computation.19 | async-start | bytes 442368
  486.0 5.6 copy-start.27
  487.9 263.0 %reduce-scatter.28.cloned.1.call-start = ((), (), s32[]{:S(2)}) async-start(), calls=%async_computation.17 | async-start | bytes 442368
  491.6 7.4 copy-start.28
  495.4 319.9 %reduce-scatter.30.cloned.1.call-start = ((), (), s32[]{:S(2)}) async-start(), calls=%async_computation.18 | async-start | bytes 442368
  502.7 56.4 %copy-start.34 = (f32[768]{0:T(1024)S(1)}, f32[768]{0:T(1024)}, u32[]{:S(2)}) copy-start(f32[768]{0:T(1024)} %get-tuple-element.234) | copy-start | bytes 9220
  502.8 56.4 %copy-start.35 = (f32[768]{0:T(1024)S(1)}, f32[768]{0:T(1024)}, u32[]{:S(2)}) copy-start(f32[768]{0:T(1024)} %get-tuple-element.239) | copy-start | bytes 9220
  502.8 56.3 %copy-start.36 = (f32[768]{0:T(1024)S(1)}, f32[768]{0:T(1024)}, u32[]{:S(2)}) copy-start(f32[768]{0:T(1024)} %get-tuple-element.232) | copy-start | bytes 9220
  502.8 56.3 %copy-start.37 = (f32[768]{0:T(1024)S(1)}, f32[768]{0:T(1024)}, u32[]{:S(2)}) copy-start(f32[768]{0:T(1024)} %get-tuple-element.237) | copy-start | bytes 9220
  502.8 351.8 %copy-start.9 = (f32[512,768]{1,0:T(8,128)S(1)}, f32[512,768]{1,0:T(8,128)}, u32[]{:S(2)}) copy-start(f32[512,768]{1,0:T(8,128)} %copy-done.8) | copy-start | bytes 4718596
  502.8 351.8 %reduce-scatter.22.cloned.1.call-start = ((), (), s32[]{:S(2)}) async-start(), calls=%async_computation.14 | async-start | bytes 3932160 | tf_op jit(solution)/shard_map/reduce_scatter | solution.py:254
  502.9 354.2 %copy-start.1 = (bf16[768,768]{1,0:T(8,128)(2,1)S(1)}, bf16[768,768]{1,0:T(8,128)(2,1)}, u32[]{:S(2)}) copy-start(bf16[768,768]{1,0:T(8,128)(2,1)} %param.35) | copy-start | bytes 3538948
  (37 other events, 89.9 us)
Sparse Core Ops, SparseCore 0:
  59.0 122.2 all-reduce.3
  216.6 59.0 reduce-scatter.17
  283.9 28.4 all-gather.2
  326.4 58.8 reduce-scatter.19
  393.5 28.4 all-gather.4
  425.3 64.8 reduce-scatter.25
  493.7 63.7 reduce-scatter.23
  560.7 61.2 reduce-scatter.33
  625.2 61.2 reduce-scatter.31
  689.7 61.1 reduce-scatter.27
  754.1 61.1 reduce-scatter.29
  817.7 36.8 reduce-scatter.21
where the time goes:
time: 869 us; the launch traced here: 864 us
  waiting for transfers between devices  554 us (64%)
  matrix products  144 us (17%)
  blocking collectives  62.6 us (7%)
  other arithmetic  50.2 us (6%)
  local copies, waits for them, and re-layouts  36.9 us (4%)
  between operations  15 us (2%)
    unnamed x16, waiting for transfers between devices  189 us
    psum x1, waiting for transfers between devices, on_device(): branch = lax.psum(matmul(context, w_out), 'tensor')  122 us
    reduce_scatter x1, waiting for transfers between devices, on_device(): lax.psum_scatter(matmul(lax.slice_in_dim(active, 0, lax.axis_size('tensor...  59.2 us
    reduce_scatter x1, waiting for transfers between devices, on_device(): lax.psum_scatter(matmul_nt(lax.slice_in_dim(grad_up_low, 0, lax.axis_size...  58.2 us
    reduce_scatter x1, waiting for transfers between devices, on_device(): lax.psum_scatter(grad_w_up.astype(jnp.bfloat16), 'dp', scatter_dimension=...  45.3 us
    psum x1, blocking collectives, on_device(): lax.psum((grad_b_out, grad_gain_one, grad_shift_one, grad_b_down, grad_ga...  40.7 us
    dot_general x14, matrix products, matmul_nt(): lax.dot_general(left, right, (((1,), (1,)), ((), ())), preferred_element_...  39.6 us
    reduce_scatter x1, waiting for transfers between devices, on_device(): lax.psum_scatter((matmul_nt(part_query, w_query) + matmul_nt(key_low, w_k...  37.7 us
  transfers between devices with their start and end apart: 12, of which 11 were waited for; matrix products, arithmetic and copies ran while one was open for 12% of the time, Pallas kernels for 0%

commit v1 on v0

v1 whole, which is shorter than its diff:
```python
import jax
import jax.numpy as jnp
from jax import lax
from jax.sharding import PartitionSpec as P

D = 768
HEADS = 12
HEAD_DIM = D // HEADS

EPS = 1e-06
NEG = -1e30
ROOT_HALF = 0.7071067811865476
INV_ROOT_TWO_PI = 0.3989422804014327
BF16 = jnp.bfloat16
F32 = jnp.float32


def matmul(left, right):
    return jnp.dot(left, right, preferred_element_type=F32)


def matmul_tn(left, right):
    return lax.dot_general(left, right, (((0,), (0,)), ((), ())), preferred_element_type=F32)


def matmul_nt(left, right):
    return lax.dot_general(left, right, (((1,), (1,)), ((), ())), preferred_element_type=F32)


def normalize(values):
    centre = values - jnp.mean(values, axis=-1, keepdims=True)
    inverse = lax.rsqrt(jnp.mean(centre * centre, axis=-1, keepdims=True) + EPS)
    return (centre * inverse, inverse)


def norm_back(upstream, normed, inverse, gain):
    shaped = upstream * gain
    centred = jnp.mean(shaped, axis=-1, keepdims=True)
    aligned = jnp.mean(shaped * normed, axis=-1, keepdims=True)
    return inverse * (shaped - centred - normed * aligned)


def visible(blocks, link_table):
    count = link_table.shape[0]
    numbers = lax.iota(jnp.int32, count)
    same_block = numbers[:, None] == numbers[None, :]
    earlier = (numbers[:, None] > numbers[None, :]) & (link_table == 1)
    table = (same_block | earlier).astype(F32)
    onehot = (blocks[:, None] == numbers[None, :]).astype(F32)
    return matmul_nt(matmul(onehot, table), onehot) > 0.5


def split_heads(tensor):
    return tensor.reshape(tensor.shape[0], tensor.shape[1] // HEAD_DIM, HEAD_DIM)


def attend_forward(query, key, value, allowed, scale):
    query, key, value = (split_heads(tensor) for tensor in (query, key, value))
    raw = jnp.einsum("qhd,khd->hqk", query, key, preferred_element_type=F32) * scale
    scores = jnp.where(allowed[None], raw, NEG)
    highest = jnp.max(scores, axis=-1, keepdims=True)
    exponent = jnp.exp(scores - highest)
    summed = jnp.sum(exponent, axis=-1, keepdims=True)
    weights = (exponent / summed).astype(BF16)
    mixed = jnp.einsum("hqk,khd->qhd", weights, value, preferred_element_type=F32)
    return (
        mixed.reshape(query.shape[0], -1).astype(BF16),
        (highest + jnp.log(summed))[:, :, 0],
    )


def attend_backward(query, key, value, grad_context, log_totals, allowed, scale):
    query, key, value, grad = (split_heads(tensor) for tensor in (query, key, value, grad_context))
    length = query.shape[0]
    raw = jnp.einsum("qhd,khd->hqk", query, key, preferred_element_type=F32) * scale
    scores = jnp.where(allowed[None], raw, NEG)
    probs = jnp.exp(scores - log_totals[:, :, None])
    pulled = jnp.einsum("qhd,khd->hqk", grad, value, preferred_element_type=F32)
    centre = jnp.sum(pulled * probs, axis=-1, keepdims=True)
    score_grad = (probs * (pulled - centre)).astype(BF16)
    grad_query = (
        jnp.einsum("hqk,khd->qhd", score_grad, key, preferred_element_type=F32) * scale
    )
    grad_key = (
        jnp.einsum("hqk,qhd->khd", score_grad, query, preferred_element_type=F32) * scale
    )
    grad_value = jnp.einsum(
        "hqk,qhd->khd", probs.astype(BF16), grad, preferred_element_type=F32
    )
    return tuple(t.reshape(length, -1) for t in (grad_query, grad_key, grad_value))


def swap_tensor(array, mask):
    ways = lax.axis_size("tensor")
    return lax.ppermute(array, "tensor", [(i, i ^ mask) for i in range(ways)])


def swap_dp(array, mask):
    ways = lax.axis_size("dp")
    return lax.ppermute(array, "dp", [(i, i ^ mask) for i in range(ways)])


def across(array):
    return swap_tensor(array, 2)


def partner(array):
    return swap_tensor(array, 1)


def scatter_rows(grad):
    ways = lax.axis_size("dp")
    pieces = lax.all_to_all(
        grad.reshape(ways, grad.shape[0] // ways, grad.shape[1]), "dp", 0, 0
    )
    return jnp.sum(pieces.astype(F32), axis=0)


def on_device(
    layer_in,
    block_of,
    block_links,
    w_query,
    b_query,
    w_key,
    w_value,
    b_value,
    w_out,
    b_out,
    gain_one,
    shift_one,
    w_up,
    b_up,
    w_down,
    b_down,
    gain_two,
    shift_two,
    grad_out,
):
    length = block_of.shape[1]
    half = length // 2
    place = lax.axis_index("tensor")
    sequence = place // 2
    core = place % 2
    scale = float(HEAD_DIM) ** (-0.5)
    width = w_query.shape[1]
    hidden = w_up.shape[1]

    qkv_mine = jnp.concatenate([w_query, w_key, w_value], axis=1)
    small_mine = jnp.concatenate([b_query, b_value, b_up])
    qkv_other = across(qkv_mine)
    small_other = across(small_mine)
    out_other = across(w_out)
    up_other = across(w_up)
    down_other = across(w_down)

    tokens = lax.dynamic_slice_in_dim(layer_in, sequence * length, length, 0)
    tokens_mine = lax.dynamic_slice_in_dim(tokens, core * half, half, 0).astype(F32)
    blocks = lax.dynamic_index_in_dim(block_of, sequence, 0, keepdims=False)
    links = lax.dynamic_index_in_dim(block_links, sequence, 0, keepdims=False)
    allowed = visible(blocks, links)

    def project(weights, bias_query, bias_value):
        all_three = matmul(tokens, weights)
        query = (all_three[:, :width] + bias_query).astype(BF16)
        key = all_three[:, width : 2 * width].astype(BF16)
        value = (all_three[:, 2 * width :] + bias_value).astype(BF16)
        return query, key, value

    heads_mine = project(qkv_mine, b_query, b_value)
    context_mine, totals_mine = attend_forward(*heads_mine, allowed, scale)
    heads_other = project(qkv_other, small_other[:width], small_other[width : 2 * width])
    context_other, totals_other = attend_forward(*heads_other, allowed, scale)
    context = jnp.concatenate([context_mine, context_other], axis=1)
    out_both = jnp.concatenate([w_out, out_other], axis=0)

    far = lax.dynamic_slice_in_dim(context, (1 - core) * half, half, 0)
    near = lax.dynamic_slice_in_dim(context, core * half, half, 0)
    branch = matmul(near, out_both) + partner(matmul(far, out_both).astype(BF16)).astype(F32)
    normed_one, inverse_one = normalize(tokens_mine + branch + b_out)
    hidden_one = normed_one * gain_one + shift_one
    hidden_low_mine = hidden_one.astype(BF16)
    hidden_low = jnp.concatenate([hidden_low_mine, partner(hidden_low_mine)], axis=0)

    def rise(weights, bias):
        up = matmul(hidden_low, weights) + bias
        phi = 0.5 * (1.0 + lax.erf(up * ROOT_HALF))
        slope = phi + up * INV_ROOT_TWO_PI * jnp.exp(-0.5 * up * up)
        return (up * phi).astype(BF16), slope

    active_mine, slope_mine = rise(w_up, b_up)
    active_other, slope_other = rise(up_other, small_other[2 * width :])
    ffn_terms = matmul(active_mine, w_down) + matmul(active_other, down_other)
    ffn = ffn_terms[:half] + partner(ffn_terms[half:].astype(BF16)).astype(F32)
    normed_two, inverse_two = normalize(hidden_one + ffn + b_down)
    layer_out = (normed_two * gain_two + shift_two).astype(BF16)

    upstream = grad_out.astype(F32)
    grad_gain_two = jnp.sum(upstream * normed_two, axis=0)
    grad_shift_two = jnp.sum(upstream, axis=0)
    grad_two = norm_back(upstream, normed_two, inverse_two, gain_two)
    grad_b_down = jnp.sum(grad_two, axis=0)
    ffn_grad_mine = grad_two.astype(BF16)
    ffn_grad = jnp.concatenate([ffn_grad_mine, partner(ffn_grad_mine)], axis=0)

    grad_up_other = matmul_nt(ffn_grad, down_other) * slope_other
    grad_up_mine = matmul_nt(ffn_grad, w_down) * slope_mine
    up_low_other = grad_up_other.astype(BF16)
    up_low_mine = grad_up_mine.astype(BF16)
    hidden_terms = matmul_nt(up_low_mine, w_up) + matmul_nt(up_low_other, up_other)
    grad_hidden = grad_two + hidden_terms[:half] + partner(
        hidden_terms[half:].astype(BF16)
    ).astype(F32)

    down_sum = matmul_tn(ffn_grad, active_mine) + across(
        matmul_tn(ffn_grad, active_other).astype(BF16)
    ).astype(F32)
    up_sum = matmul_tn(hidden_low, up_low_mine) + across(
        matmul_tn(hidden_low, up_low_other).astype(BF16)
    ).astype(F32)
    grad_w_down = scatter_rows(down_sum.astype(BF16)).T
    grad_w_up = scatter_rows(up_sum.astype(BF16))

    grad_gain_one = jnp.sum(grad_hidden * normed_one, axis=0)
    grad_shift_one = jnp.sum(grad_hidden, axis=0)
    grad_one = norm_back(grad_hidden, normed_one, inverse_one, gain_one)
    grad_b_out = jnp.sum(grad_one, axis=0)
    one_low = grad_one.astype(BF16)
    one_partner = partner(one_low)
    pair = jnp.concatenate([one_low, one_partner, one_low], axis=0)
    branch_grad = lax.dynamic_slice_in_dim(pair, core * half, length, 0)
    grad_context = matmul_nt(branch_grad, out_both).astype(BF16)
    out_sum = matmul_tn(branch_grad, context_mine) + across(
        matmul_tn(branch_grad, context_other).astype(BF16)
    ).astype(F32)

    row_sums = jnp.stack(
        [grad_b_out, grad_gain_one, grad_shift_one, grad_b_down, grad_gain_two, grad_shift_two]
    )
    row_sums = row_sums + partner(row_sums)
    row_sums = row_sums + across(row_sums)
    hidden_sums = jnp.sum(grad_up_mine, axis=0) + across(jnp.sum(grad_up_other, axis=0))
    sums = jnp.concatenate([row_sums, hidden_sums.reshape(-1, D)], axis=0)
    mask = 1
    while mask < lax.axis_size("dp"):
        sums = sums + swap_dp(sums, mask)
        mask = mask * 2

    grads_other = attend_backward(
        *heads_other, grad_context[:, width:], totals_other, allowed, scale
    )
    grads_mine = attend_backward(
        *heads_mine, grad_context[:, :width], totals_mine, allowed, scale
    )
    low_other = jnp.concatenate(grads_other, axis=1).astype(BF16)
    low_mine = jnp.concatenate(grads_mine, axis=1).astype(BF16)
    bias_mine = jnp.concatenate([jnp.sum(grads_mine[0], axis=0), jnp.sum(grads_mine[2], axis=0)])
    bias_other = jnp.concatenate(
        [jnp.sum(grads_other[0], axis=0), jnp.sum(grads_other[2], axis=0)]
    )
    bias_sums = bias_mine + across(bias_other)
    qkv_sum = matmul_tn(tokens, low_mine) + across(
        matmul_tn(tokens, low_other).astype(BF16)
    ).astype(F32)

    in_terms = matmul_nt(low_mine, qkv_mine) + matmul_nt(low_other, qkv_other)
    in_far = lax.dynamic_slice_in_dim(in_terms, (1 - core) * half, half, 0)
    in_near = lax.dynamic_slice_in_dim(in_terms, core * half, half, 0)
    grad_in = grad_one + in_near + partner(in_far.astype(BF16)).astype(F32)

    mask = 1
    while mask < lax.axis_size("dp"):
        bias_sums = bias_sums + swap_dp(bias_sums, mask)
        mask = mask * 2
    attention = jnp.concatenate([qkv_sum, out_sum], axis=1).astype(BF16)
    attention = scatter_rows(attention)

    return (
        layer_out,
        grad_in,
        attention[:, :width],
        bias_sums[:width],
        attention[:, width : 2 * width],
        attention[:, 2 * width : 3 * width],
        bias_sums[width:],
        attention[:, 3 * width :].T,
        sums[0],
        sums[1],
        sums[2],
        grad_w_up,
        sums[6:].reshape(-1),
        grad_w_down,
        sums[3],
        sums[4],
        sums[5],
    )


def solution(mesh):
    in_specs = (
        P("dp", None),
        P("dp", None),
        P("dp", None, None),
        P(None, "tensor"),
        P("tensor"),
        P(None, "tensor"),
        P(None, "tensor"),
        P("tensor"),
        P("tensor", None),
        P(),
        P(),
        P(),
        P(None, "tensor"),
        P("tensor"),
        P("tensor", None),
        P(),
        P(),
        P(),
        P(("dp", "tensor"), None),
    )
    out_specs = (
        P(("dp", "tensor"), None),
        P(("dp", "tensor"), None),
        P("dp", "tensor"),
        P("tensor"),
        P("dp", "tensor"),
        P("dp", "tensor"),
        P("tensor"),
        P("tensor", "dp"),
        P(),
        P(),
        P(),
        P("dp", "tensor"),
        P("tensor"),
        P("tensor", "dp"),
        P(),
        P(),
        P(),
    )
    return jax.shard_map(
        on_device, mesh=mesh, in_specs=in_specs, out_specs=out_specs, check_vma=False
    )
```

time: 869 us -> 329 us (0.38)
  waiting for transfers between devices: 554 us -> 120 us
  blocking collectives: 62.6 us -> 0 us
  matrix products: 144 us -> 97.9 us
  starting transfers between devices: 0.9 us -> 40.9 us
  between operations: 15 us -> 2.19 us
  local copies, waits for them, and re-layouts: 36.9 us -> 25.4 us
  other arithmetic: 50.2 us -> 39.7 us
    reduce_scatter x5 -> x0, waiting for transfers between devices: 200 us -> none  [the longest x1 59.2 us: on_device(): lax.psum_scatter(matmul(lax.slice_in_dim(active, 0, lax.axis_size('tensor...]
    unnamed x16 -> x0, waiting for transfers between devices: 189 us -> none
    psum x1 -> x0, waiting for transfers between devices: 122 us -> none  [on_device(): branch = lax.psum(matmul(context, w_out), 'tensor')]
    ppermute x0 -> x26, waiting for transfers between devices: none -> 118 us  [the longest x20 100 us: swap_tensor(): return lax.ppermute(array, 'tensor', [(i, i ^ mask) for i in range(ways)])]
    psum x2 -> x0, blocking collectives: 62.6 us -> none  [the longest x1 40.7 us: on_device(): lax.psum((grad_b_out, grad_gain_one, grad_shift_one, grad_b_down, grad_ga...]
    all_gather x2 -> x0, waiting for transfers between devices: 42.1 us -> none  [the longest x1 28.6 us: on_device(): lax.all_gather(grad_two.astype(jnp.bfloat16), 'tensor', axis=0, tiled=True)]
    dot_general x34 -> x20, matrix products: 80.7 us -> 55.8 us  [the longest x8 14.2 us: matmul(): return jnp.dot(left, right, preferred_element_type=F32)]
    ppermute x0 -> x26, starting transfers between devices: none -> 24.6 us  [the longest x20 14.7 us: swap_tensor(): return lax.ppermute(array, 'tensor', [(i, i ^ mask) for i in range(ways)])]
  transfers between devices with their start and end apart: 12 -> 29, of which waited for: 11 -> 13; matrix products, arithmetic and copies ran while one was open for 12% -> 38% of each run, Pallas kernels for 0% -> 0%
where the time goes in v1:
time: 329 us; the launch traced here: 326 us
  waiting for transfers between devices  120 us (36%)
  matrix products  97.9 us (30%)
  starting transfers between devices  40.9 us (12%)
  other arithmetic  39.7 us (12%)
  local copies, waits for them, and re-layouts  25.4 us (8%)
    ppermute x20, waiting for transfers between devices, swap_tensor(): return lax.ppermute(array, 'tensor', [(i, i ^ mask) for i in range(ways)])  100 us
    dot_general x8, matrix products, matmul_tn(): lax.dot_general(left, right, (((0,), (0,)), ((), ())), preferred_element_...  22.1 us
    dot_general x8, matrix products, matmul_nt(): lax.dot_general(left, right, (((1,), (1,)), ((), ())), preferred_element_...  20 us
    ppermute x6, waiting for transfers between devices, swap_dp(): return lax.ppermute(array, 'dp', [(i, i ^ mask) for i in range(ways)])  18.2 us
    all_to_all x3, starting transfers between devices, scatter_rows(): lax.all_to_all(grad.reshape(ways, grad.shape[0] // ways, grad.shape[1]),...  16.2 us
    convert_element_type x2, other arithmetic, attend_backward(): score_grad = (probs * (pulled - centre)).astype(BF16)  15.1 us
    ppermute x20, starting transfers between devices, swap_tensor(): return lax.ppermute(array, 'tensor', [(i, i ^ mask) for i in range(ways)])  14.7 us
    dot_general x8, matrix products, matmul(): return jnp.dot(left, right, preferred_element_type=F32)  14.2 us
  transfers between devices with their start and end apart: 29, of which 13 were waited for; matrix products, arithmetic and copies ran while one was open for 38% of the time, Pallas kernels for 0%

profile of v1, /device:TPU:0, one launch (start us, length us, event | category | flops | bytes accessed | tf_op | source)
XLA Modules:
  0.0 325.9 jit_solution(1645924724197972133)
XLA Ops:
  1.5 3.0 collective-permute-start.1
  11.5 2.8 fusion.53
  18.4 3.2 fusion.115
  23.5 2.9 copy-done.2
  35.2 3.2 fusion.116
  40.3 2.8 copy-done.3
  57.1 23.8 %collective-permute-done.5 = bf16[768,768]{1,0:T(8,128)(2,1)S(1)} collective-permute-done((bf16[768,768]{1,0:T(8,128)(2,1)S(1)}, bf16[768,768]{1,0:T(8,128)(2,1)S(1)}, u32[]{:S(2)}, u32[]{:S(2)}) %collective-permute-start.5) | collective-permute-done | bytes 1179680 | tf_op jit(solution)/shard_map/ppermute | solution.py:95
  82.5 22.9 %collective-permute-done.6 = bf16[768,768]{1,0:T(8,128)(2,1)S(1)} collective-permute-done((bf16[768,768]{1,0:T(8,128)(2,1)S(1)}, bf16[768,768]{1,0:T(8,128)(2,1)S(1)}, u32[]{:S(2)}, u32[]{:S(2)}) %collective-permute-start.6) | collective-permute-done | bytes 1179680 | tf_op jit(solution)/shard_map/ppermute | solution.py:95
  115.1 3.2 fusion.118
  119.8 3.7 %fusion.119 = (f32[768]{0:T(1024)S(1)}, bf16[1024,768]{1,0:T(8,128)(2,1)S(1)}) fusion(f32[1024,768]{1,0:T(8,128)S(1)} %get-tuple-element.122, f32[768]{0:T(1024)S(1)} %slice.124, bf16[768,768]{1,0:T(8,128)(2,1)S(1)} %collective-permute-done.6, bf16[512,768]{1,0:T(8,128)(2,1)S(1)} %collective-permute-done.8, bf16[512,768]{1,0:T(8,128)(2,1)S(1)} %convert_element_type.169), kind=kOutput, calls=%fused_computation.203 | convolution fusion | flops 1220541696 | bytes 7477248 | tf_op jit(solution)/shard_map/dot_general | solution.py:27
  137.3 44.6 %collective-permute-done.20 = f32[768]{0:T(1024)S(1)} collective-permute-done((f32[768]{0:T(1024)S(1)}, f32[768]{0:T(1024)S(1)}, u32[]{:S(2)}, u32[]{:S(2)}) %collective-permute-start.20) | collective-permute-done | bytes 3104 | tf_op jit(solution)/shard_map/ppermute | solution.py:95
  184.9 3.7 %add_convert_fusion.1 = bf16[768,768]{1,0:T(8,128)(2,1)} fusion(bf16[768,768]{1,0:T(8,128)(2,1)} %collective-permute-done.24, bf16[1024,768]{1,0:T(8,128)(2,1)S(1)} %copy-done.66, bf16[512,768]{1,0:T(8,128)(2,1)S(1)} %copy-done.61, bf16[512,768]{1,0:T(8,128)(2,1)S(1)} %fusion.32), kind=kOutput, calls=%fused_computation.45 | convolution fusion | flops 1212874752 | bytes 5505024 | tf_op jit(solution)/shard_map/dot_general | solution.py:23
  188.6 5.2 %all-to-all-start.1 = ((bf16[8,96,768]{2,1,0:T(8,128)(2,1)}), bf16[8,96,768]{2,1,0:T(8,128)(2,1)}, u32[]{:S(2)}, u32[]{:S(2)}) async-start(bf16[8,96,768]{2,1,0:T(8,128)(2,1)} %bitcast.121), calls=%async_computation.1 | async-start | bytes 2359296 | tf_op jit(solution)/shard_map/all_to_all | solution.py:113
  193.9 4.6 %add_convert_fusion = bf16[768,768]{1,0:T(8,128)(2,1)} fusion(bf16[768,768]{1,0:T(8,128)(2,1)} %collective-permute-done.25, bf16[1024,768]{1,0:T(8,128)(2,1)} %copy-done.64, bf16[512,768]{1,0:T(8,128)(2,1)} %copy-done.62, bf16[512,768]{1,0:T(8,128)(2,1)S(1)} %copy-done.27), kind=kOutput, calls=%fused_computation.43 | convolution fusion | flops 1212874752 | bytes 5505024 | tf_op jit(solution)/shard_map/dot_general | solution.py:23
  198.6 3.6 %fusion.27 = bf16[1024,768]{1,0:T(8,128)(2,1)S(1)} fusion(s32[]{:T(128)S(6)} %select_n.55, bf16[512,768]{1,0:T(8,128)(2,1)S(1)} %copy-done.14, bf16[512,768]{1,0:T(8,128)(2,1)} %collective-permute-done.10), kind=kLoop, calls=%fused_computation.59 | loop fusion | flops 4718592 | bytes 3145732 | tf_op jit(solution)/shard_map/concatenate | solution.py:230
  205.0 3.8 %fusion.111 = (f32[3,64]{1,0:T(4,128)S(1)}, bf16[1024,3,64]{0,2,1:T(8,128)(2,1)}) fusion(bf16[1024,3,64]{0,2,1:T(8,128)(2,1)} %bitcast.19, f32[3,1024,1024]{1,2,0:T(8,128)S(1)} %bitcast.97, f32[3,1024]{1,0:T(4,128)S(1)} %copy-done.25), kind=kOutput, calls=%fused_computation.195 | convolution fusion | flops 409337664 | bytes 13382400 | tf_op jit(solution)/shard_map/hqk,qhd->khd/dot_general | solution.py:87
  208.8 3.9 %multiply_reduce_fusion = (f32[3,1024]{1,0:T(4,128)S(1)}, f32[3,1024,1024]{1,2,0:T(8,128)S(1)}) fusion(f32[3,1024,1024]{1,2,0:T(8,128)S(1)} %bitcast.97, f32[3,1024]{1,0:T(4,128)S(1)} %copy-done.25, bf16[1024,3,64]{0,2,1:T(8,128)(2,1)} %bitcast.19, bf16[1024,3,64]{0,2,1:T(8,128)(2,1)} %bitcast.112), kind=kOutput, calls=%fused_computation.1 | convolution fusion | flops 412087296 | bytes 25976832 | tf_op jit(solution)/shard_map/qhd,khd->hqk/dot_general | solution.py:78
  213.4 5.4 %multiply_convert_fusion = bf16[3,1024,1024]{1,2,0:T(8,128)(2,1)} fusion(f32[3,1024,1024]{1,2,0:T(8,128)S(1)} %get-tuple-element.126, f32[3,1024,1024]{1,2,0:T(8,128)S(1)} %bitcast.97, f32[3,1024]{1,0:T(4,128)S(1)} %get-tuple-element.125, f32[3,1024]{1,0:T(4,128)S(1)} %copy-done.25), kind=kLoop, calls=%fused_computation | loop fusion | flops 12582912 | bytes 31481856 | tf_op jit(solution)/shard_map/convert_element_type | solution.py:80
  218.9 5.0 %fusion.42 = bf16[3,64,1024]{2,1,0:T(8,128)(2,1)S(1)} fusion(bf16[1024,3,64]{0,2,1:T(8,128)(2,1)S(1)} %bitcast.104, bf16[3,1024,1024]{1,2,0:T(8,128)(2,1)} %multiply_convert_fusion), kind=kOutput, calls=%fused_computation.98 | convolution fusion | flops 403046400 | bytes 7077888 | tf_op jit(solution)/shard_map/hqk,qhd->khd/dot_general | solution.py:85
  223.9 4.2 %fusion.110 = (f32[3,64]{1,0:T(4,128)S(1)}, bf16[1024,3,64]{0,2,1:T(8,128)(2,1)S(1)}) fusion(bf16[1024,3,64]{0,2,1:T(8,128)(2,1)S(1)} %bitcast.108, bf16[3,1024,1024]{1,2,0:T(8,128)(2,1)} %multiply_convert_fusion), kind=kOutput, calls=%fused_computation.194 | convolution fusion | flops 403242816 | bytes 7078656 | tf_op jit(solution)/shard_map/hqk,khd->qhd/dot_general | solution.py:82
  231.8 2.8 fusion.109
  234.6 6.6 %multiply_reduce_fusion.1 = (f32[3,1024]{1,0:T(4,128)}, f32[3,1024,1024]{1,2,0:T(8,128)}) fusion(f32[3,1024,1024]{1,2,0:T(8,128)S(1)} %bitcast.95, f32[3,1024]{1,0:T(4,128)S(1)} %copy-done.23, bf16[1024,3,64]{0,2,1:T(8,128)(2,1)S(1)} %bitcast.99, bf16[1024,3,64]{0,2,1:T(8,128)(2,1)S(1)} %bitcast.110), kind=kOutput, calls=%fused_computation.4 | convolution fusion | flops 412087296 | bytes 25976832 | tf_op jit(solution)/shard_map/qhd,khd->hqk/dot_general | solution.py:78
  241.2 6.4 %all-to-all-start.2 = ((bf16[8,96,768]{2,1,0:T(8,128)(2,1)}), bf16[8,96,768]{2,1,0:T(8,128)(2,1)}, u32[]{:S(2)}, u32[]{:S(2)}) async-start(bf16[8,96,768]{2,1,0:T(8,128)(2,1)} %bitcast.120), calls=%async_computation.2 | async-start | bytes 2359296 | tf_op jit(solution)/shard_map/all_to_all | solution.py:113
  247.7 9.7 %multiply_convert_fusion.1 = bf16[3,1024,1024]{1,2,0:T(8,128)(2,1)S(1)} fusion(f32[3,1024,1024]{1,2,0:T(8,128)} %get-tuple-element.124, f32[3,1024,1024]{1,2,0:T(8,128)} %copy-done.2, f32[3,1024]{1,0:T(4,128)S(1)} %copy-done.43, f32[3,1024]{1,0:T(4,128)S(1)} %copy-done.24), kind=kLoop, calls=%fused_computation.3 | loop fusion | flops 12582912 | bytes 31481856 | tf_op jit(solution)/shard_map/convert_element_type | solution.py:80
  261.3 4.4 %fusion.66 = f32[1024,768]{1,0:T(8,128)} fusion(bf16[768,576]{0,1:T(8,128)(2,1)} %constant_dynamic-update-slice_fusion, bf16[1024,192]{0,1:T(8,128)(2,1)S(1)} %bitcast.125, bf16[1024,192]{0,1:T(8,128)(2,1)S(1)} %bitcast.128, bf16[1024,192]{0,1:T(8,128)(2,1)S(1)} %bitcast.132), kind=kOutput, calls=%fused_computation.135 | convolution fusion | flops 909508608 | bytes 5210112 | tf_op jit(solution)/shard_map/dot_general | solution.py:27
  267.4 4.0 %add_convert_fusion.2 = bf16[768,576]{0,1:T(8,128)(2,1)} fusion(bf16[768,576]{0,1:T(8,128)(2,1)} %collective-permute-done.12, bf16[2048,768]{1,0:T(8,128)(2,1)} %param.19, s32[]{:T(128)S(6)} %select_n.49, bf16[1024,192]{0,1:T(8,128)(2,1)} %bitcast.124, bf16[1024,192]{0,1:T(8,128)(2,1)} %bitcast.129, bf16[1024,192]{0,1:T(8,128)(2,1)} %bitcast.133), kind=kOutput, calls=%fused_computation.52 | convolution fusion | flops 910835712 | bytes 4521988 | tf_op jit(solution)/shard_map/dot_general | solution.py:23
  275.6 4.6 %all-to-all-start = ((bf16[8,96,768]{2,1,0:T(8,128)(2,1)}), bf16[8,96,768]{2,1,0:T(8,128)(2,1)S(1)}, u32[]{:S(2)}, u32[]{:S(2)}) async-start(bf16[8,96,768]{2,1,0:T(8,128)(2,1)} %pad_maximum_fusion.4), calls=%async_computation | async-start | bytes 2359296 | tf_op jit(solution)/shard_map/all_to_all | solution.py:113
  280.2 3.9 %convolution_add_fusion = f32[1024,768]{1,0:T(8,128)S(1)} fusion(f32[1024,768]{1,0:T(8,128)} %fusion.66, bf16[768,576]{0,1:T(8,128)(2,1)} %collective-permute-done, bf16[1024,192]{0,1:T(8,128)(2,1)S(1)} %bitcast.123, bf16[1024,192]{0,1:T(8,128)(2,1)} %bitcast.127, bf16[1024,192]{0,1:T(8,128)(2,1)} %bitcast.131), kind=kOutput, calls=%fused_computation.51 | convolution fusion | flops 910295040 | bytes 8355840 | tf_op jit(solution)/shard_map/dot_general | solution.py:27
  290.4 8.5 %collective-permute-done.22 = f32[7,768]{1,0:T(8,128)S(1)} collective-permute-done((f32[7,768]{1,0:T(8,128)S(1)}, f32[7,768]{1,0:T(8,128)S(1)}, u32[]{:S(2)}, u32[]{:S(2)}) %collective-permute-start.22) | collective-permute-done | bytes 21536 | tf_op jit(solution)/shard_map/ppermute | solution.py:100
  298.9 5.0 %collective-permute-start.23 = (f32[7,768]{1,0:T(8,128)S(1)}, f32[7,768]{1,0:T(8,128)S(1)}, u32[]{:S(2)}, u32[]{:S(2)}) collective-permute-start(f32[7,768]{1,0:T(8,128)S(1)} %add.282), channel_id=1, source_target_pairs={{0,16},{4,20},{8,24},{12,28},{16,0},{20,4},{24,8},{28,12},{1,17},{... | collective-permute-start | bytes 64520 | tf_op jit(solution)/shard_map/ppermute | solution.py:100
  312.0 3.8 %collective-permute-done.17 = f32[384]{0:T(512)S(1)} collective-permute-done((f32[384]{0:T(512)S(1)}, f32[384]{0:T(512)S(1)}, u32[]{:S(2)}, u32[]{:S(2)}) %collective-permute-start.17) | collective-permute-done | bytes 1568 | tf_op jit(solution)/shard_map/ppermute | solution.py:100
  316.4 3.2 convert_add_fusion
  (287 shorter events, 105.4 us)
Async XLA Ops:
  1.5 27.4 %collective-permute-start.1 = (f32[1152]{0:T(1024)S(1)}, f32[1152]{0:T(1024)S(1)}, u32[]{:S(2)}, u32[]{:S(2)}) collective-permute-start(f32[1152]{0:T(1024)S(1)} %concatenate.48), channel_id=1, source_target_pairs={{0,2},{1,3},{2,0},{3,1},{4,6},{5,7},{6,4},{7,5},{8,10},{9,11},{10,... | collective-permute-start | bytes 13832 | tf_op jit(solution)/shard_map/ppermute | solution.py:95
  4.4 24.5 %collective-permute-start.2 = (bf16[192,768]{1,0:T(8,128)(2,1)}, bf16[192,768]{1,0:T(8,128)(2,1)}, u32[]{:S(2)}, u32[]{:S(2)}) collective-permute-start(bf16[192,768]{1,0:T(8,128)(2,1)} %param.27), channel_id=1, source_target_pairs={{0,2},{1,3},{2,0},{3,1},{4,6},{5,7},{6,4},{7,5},{8,10},{9,11},{10,... | collective-permute-start | bytes 884744 | tf_op jit(solution)/shard_map/ppermute | solution.py:95
  9.5 22.6 %collective-permute-start = (bf16[768,576]{0,1:T(8,128)(2,1)}, bf16[768,576]{0,1:T(8,128)(2,1)}, u32[]{:S(2)}, u32[]{:S(2)}) collective-permute-start(bf16[768,576]{0,1:T(8,128)(2,1)} %constant_dynamic-update-slice_fusion), channel_id=1, source_target_pairs={{0,2},{1,3},{2,0},{3,1},{4,6},{5,7},{6,4},{7,5},{8,10},{9,11},{10,... | collective-permute-start | bytes 2654216 | tf_op jit(solution)/shard_map/ppermute | solution.py:95
  46.4 2.4 collective-permute-start.3
  51.5 2.6 collective-permute-start.4
  52.1 28.8 %collective-permute-start.5 = (bf16[768,768]{1,0:T(8,128)(2,1)S(1)}, bf16[768,768]{1,0:T(8,128)(2,1)S(1)}, u32[]{:S(2)}, u32[]{:S(2)}) collective-permute-start(bf16[768,768]{1,0:T(8,128)(2,1)S(1)} %copy-done.59), channel_id=1, source_target_pairs={{0,2},{1,3},{2,0},{3,1},{4,6},{5,7},{6,4},{7,5},{8,10},{9,11},{10,... | collective-permute-start | bytes 3538952 | tf_op jit(solution)/shard_map/ppermute | solution.py:95
  52.6 52.8 %collective-permute-start.6 = (bf16[768,768]{1,0:T(8,128)(2,1)S(1)}, bf16[768,768]{1,0:T(8,128)(2,1)S(1)}, u32[]{:S(2)}, u32[]{:S(2)}) collective-permute-start(bf16[768,768]{1,0:T(8,128)(2,1)S(1)} %copy-done.58), channel_id=1, source_target_pairs={{0,2},{1,3},{2,0},{3,1},{4,6},{5,7},{6,4},{7,5},{8,10},{9,11},{10,... | collective-permute-start | bytes 3538952 | tf_op jit(solution)/shard_map/ppermute | solution.py:95
  54.1 71.1 %copy-start.60 = (bf16[512,768]{1,0:T(8,128)(2,1)}, bf16[512,768]{1,0:T(8,128)(2,1)S(1)}, u32[]{:S(2)}) copy-start(bf16[512,768]{1,0:T(8,128)(2,1)S(1)} %collective-permute-done.4) | copy-start | bytes 2359300
  106.9 2.4 collective-permute-start.7
  112.7 2.4 collective-permute-start.8
  125.0 7.2 %collective-permute-start.9 = (bf16[512,768]{1,0:T(8,128)(2,1)S(1)}, bf16[512,768]{1,0:T(8,128)(2,1)S(1)}, u32[]{:S(2)}, u32[]{:S(2)}) collective-permute-start(bf16[512,768]{1,0:T(8,128)(2,1)S(1)} %slice.174), channel_id=1, source_target_pairs={{0,1},{1,0},{2,3},{3,2},{4,5},{5,4},{6,7},{7,6},{8,9},{9,8},{10,11... | collective-permute-start | bytes 2359304 | tf_op jit(solution)/shard_map/ppermute | solution.py:95
  127.7 57.2 %collective-permute-start.24 = (bf16[768,768]{1,0:T(8,128)(2,1)}, bf16[768,768]{1,0:T(8,128)(2,1)}, u32[]{:S(2)}, u32[]{:S(2)}) collective-permute-start(bf16[768,768]{1,0:T(8,128)(2,1)} %convolution_convert_fusion.1), channel_id=1, source_target_pairs={{0,2},{1,3},{2,0},{3,1},{4,6},{5,7},{6,4},{7,5},{8,10},{9,11},{10,... | collective-permute-start | bytes 3538952 | tf_op jit(solution)/shard_map/ppermute | solution.py:95
  130.7 63.2 %collective-permute-start.25 = (bf16[768,768]{1,0:T(8,128)(2,1)}, bf16[768,768]{1,0:T(8,128)(2,1)}, u32[]{:S(2)}, u32[]{:S(2)}) collective-permute-start(bf16[768,768]{1,0:T(8,128)(2,1)} %convolution_convert_fusion), channel_id=1, source_target_pairs={{0,2},{1,3},{2,0},{3,1},{4,6},{5,7},{6,4},{7,5},{8,10},{9,11},{10,... | collective-permute-start | bytes 3538952 | tf_op jit(solution)/shard_map/ppermute | solution.py:95
  133.8 1.3 collective-permute-start.18
  134.5 50.4 %copy-start.61 = (bf16[512,768]{1,0:T(8,128)(2,1)S(1)}, bf16[512,768]{1,0:T(8,128)(2,1)}, u32[]{:S(2)}) copy-start(bf16[512,768]{1,0:T(8,128)(2,1)} %copy-done.60) | copy-start | bytes 2359300
  134.5 50.4 %copy-start.66 = (bf16[1024,768]{1,0:T(8,128)(2,1)S(1)}, bf16[1024,768]{1,0:T(8,128)(2,1)}, u32[]{:S(2)}) copy-start(bf16[1024,768]{1,0:T(8,128)(2,1)} %copy-done.65) | copy-start | bytes 4718596
  134.5 47.3 %collective-permute-start.20 = (f32[768]{0:T(1024)S(1)}, f32[768]{0:T(1024)S(1)}, u32[]{:S(2)}, u32[]{:S(2)}) collective-permute-start(f32[768]{0:T(1024)S(1)} %get-tuple-element.133), channel_id=1, source_target_pairs={{0,2},{1,3},{2,0},{3,1},{4,6},{5,7},{6,4},{7,5},{8,10},{9,11},{10,... | collective-permute-start | bytes 9224 | tf_op jit(solution)/shard_map/ppermute | solution.py:95
  135.1 47.0 %collective-permute-start.19 = (f32[6,768]{1,0:T(8,128)S(1)}, f32[6,768]{1,0:T(8,128)S(1)}, u32[]{:S(2)}, u32[]{:S(2)}) collective-permute-start(f32[6,768]{1,0:T(8,128)S(1)} %add.278), channel_id=1, source_target_pairs={{0,2},{1,3},{2,0},{3,1},{4,6},{5,7},{6,4},{7,5},{8,10},{9,11},{10,... | collective-permute-start | bytes 55304 | tf_op jit(solution)/shard_map/ppermute | solution.py:95
  181.9 16.6 %collective-permute-start.10 = (bf16[512,768]{1,0:T(8,128)(2,1)S(1)}, bf16[512,768]{1,0:T(8,128)(2,1)}, u32[]{:S(2)}, u32[]{:S(2)}) collective-permute-start(bf16[512,768]{1,0:T(8,128)(2,1)S(1)} %convert_element_type.173), channel_id=1, source_target_pairs={{0,1},{1,0},{2,3},{3,2},{4,5},{5,4},{6,7},{7,6},{8,9},{9,8},{10,11... | collective-permute-start | bytes 2359304 | tf_op jit(solution)/shard_map/ppermute | solution.py:95
  183.4 103.3 %collective-permute-start.21 = (f32[7,768]{1,0:T(8,128)}, f32[7,768]{1,0:T(8,128)}, u32[]{:S(2)}, u32[]{:S(2)}) collective-permute-start(f32[7,768]{1,0:T(8,128)} %pad_maximum_fusion.9), channel_id=1, source_target_pairs={{0,4},{4,0},{8,12},{12,8},{16,20},{20,16},{24,28},{28,24},{1,5},{5... | collective-permute-start | bytes 64520 | tf_op jit(solution)/shard_map/ppermute | solution.py:100
  188.6 52.5 %all-to-all-start.1 = ((bf16[8,96,768]{2,1,0:T(8,128)(2,1)}), bf16[8,96,768]{2,1,0:T(8,128)(2,1)}, u32[]{:S(2)}, u32[]{:S(2)}) async-start(bf16[8,96,768]{2,1,0:T(8,128)(2,1)} %bitcast.121), calls=%async_computation.1 | async-start | bytes 2359296 | tf_op jit(solution)/shard_map/all_to_all | solution.py:113
  212.7 53.0 %collective-permute-start.13 = (bf16[768,192]{0,1:T(8,128)(2,1)}, bf16[768,192]{0,1:T(8,128)(2,1)}, u32[]{:S(2)}, u32[]{:S(2)}) collective-permute-start(bf16[768,192]{0,1:T(8,128)(2,1)} %convolution_convert_fusion.5), channel_id=1, source_target_pairs={{0,2},{1,3},{2,0},{3,1},{4,6},{5,7},{6,4},{7,5},{8,10},{9,11},{10,... | collective-permute-start | bytes 884744 | tf_op jit(solution)/shard_map/ppermute | solution.py:95
  230.3 37.0 %collective-permute-start.12 = (bf16[768,576]{0,1:T(8,128)(2,1)}, bf16[768,576]{0,1:T(8,128)(2,1)}, u32[]{:S(2)}, u32[]{:S(2)}) collective-permute-start(bf16[768,576]{0,1:T(8,128)(2,1)} %convolution_convert_fusion.2), channel_id=1, source_target_pairs={{0,2},{1,3},{2,0},{3,1},{4,6},{5,7},{6,4},{7,5},{8,10},{9,11},{10,... | collective-permute-start | bytes 2654216 | tf_op jit(solution)/shard_map/ppermute | solution.py:95
  241.2 34.4 %all-to-all-start.2 = ((bf16[8,96,768]{2,1,0:T(8,128)(2,1)}), bf16[8,96,768]{2,1,0:T(8,128)(2,1)}, u32[]{:S(2)}, u32[]{:S(2)}) async-start(bf16[8,96,768]{2,1,0:T(8,128)(2,1)} %bitcast.120), calls=%async_computation.2 | async-start | bytes 2359296 | tf_op jit(solution)/shard_map/all_to_all | solution.py:113
  275.6 48.3 %all-to-all-start = ((bf16[8,96,768]{2,1,0:T(8,128)(2,1)}), bf16[8,96,768]{2,1,0:T(8,128)(2,1)S(1)}, u32[]{:S(2)}, u32[]{:S(2)}) async-start(bf16[8,96,768]{2,1,0:T(8,128)(2,1)} %pad_maximum_fusion.4), calls=%async_computation | async-start | bytes 2359296 | tf_op jit(solution)/shard_map/all_to_all | solution.py:113
  286.7 29.8 %collective-permute-start.11 = (bf16[512,768]{1,0:T(8,128)(2,1)}, bf16[512,768]{1,0:T(8,128)(2,1)}, u32[]{:S(2)}, u32[]{:S(2)}) collective-permute-start(bf16[512,768]{1,0:T(8,128)(2,1)} %dynamic-slice_convert_fusion), channel_id=1, source_target_pairs={{0,1},{1,0},{2,3},{3,2},{4,5},{5,4},{6,7},{7,6},{8,9},{9,8},{10,11... | collective-permute-start | bytes 2359304 | tf_op jit(solution)/shard_map/ppermute | solution.py:95
  287.4 11.5 %collective-permute-start.22 = (f32[7,768]{1,0:T(8,128)S(1)}, f32[7,768]{1,0:T(8,128)S(1)}, u32[]{:S(2)}, u32[]{:S(2)}) collective-permute-start(f32[7,768]{1,0:T(8,128)S(1)} %fusion.169), channel_id=1, source_target_pairs={{0,8},{4,12},{8,0},{12,4},{16,24},{20,28},{24,16},{28,20},{1,9},{5... | collective-permute-start | bytes 64520 | tf_op jit(solution)/shard_map/ppermute | solution.py:100
  289.8 14.3 %collective-permute-start.14 = (f32[384]{0:T(512)S(1)}, f32[384]{0:T(512)S(1)}, u32[]{:S(2)}, u32[]{:S(2)}) collective-permute-start(f32[384]{0:T(512)S(1)} %pad_maximum_fusion.10), channel_id=1, source_target_pairs={{0,2},{1,3},{2,0},{3,1},{4,6},{5,7},{6,4},{7,5},{8,10},{9,11},{10,... | collective-permute-start | bytes 4616 | tf_op jit(solution)/shard_map/ppermute | solution.py:95
  298.9 10.1 %collective-permute-start.23 = (f32[7,768]{1,0:T(8,128)S(1)}, f32[7,768]{1,0:T(8,128)S(1)}, u32[]{:S(2)}, u32[]{:S(2)}) collective-permute-start(f32[7,768]{1,0:T(8,128)S(1)} %add.282), channel_id=1, source_target_pairs={{0,16},{4,20},{8,24},{12,28},{16,0},{20,4},{24,8},{28,12},{1,17},{... | collective-permute-start | bytes 64520 | tf_op jit(solution)/shard_map/ppermute | solution.py:100
  304.1 3.6 %collective-permute-start.15 = (f32[384]{0:T(512)S(1)}, f32[384]{0:T(512)S(1)}, u32[]{:S(2)}, u32[]{:S(2)}) collective-permute-start(f32[384]{0:T(512)S(1)} %maximum_add_fusion), channel_id=1, source_target_pairs={{0,4},{4,0},{8,12},{12,8},{16,20},{20,16},{24,28},{28,24},{1,5},{5... | collective-permute-start | bytes 4616 | tf_op jit(solution)/shard_map/ppermute | solution.py:100
  307.7 3.6 %collective-permute-start.16 = (f32[384]{0:T(512)S(1)}, f32[384]{0:T(512)S(1)}, u32[]{:S(2)}, u32[]{:S(2)}) collective-permute-start(f32[384]{0:T(512)S(1)} %add.275), channel_id=1, source_target_pairs={{0,8},{4,12},{8,0},{12,4},{16,24},{20,28},{24,16},{28,20},{1,9},{5... | collective-permute-start | bytes 4616 | tf_op jit(solution)/shard_map/ppermute | solution.py:100
  311.3 4.5 %collective-permute-start.17 = (f32[384]{0:T(512)S(1)}, f32[384]{0:T(512)S(1)}, u32[]{:S(2)}, u32[]{:S(2)}) collective-permute-start(f32[384]{0:T(512)S(1)} %add.276), channel_id=1, source_target_pairs={{0,16},{4,20},{8,24},{12,28},{16,0},{20,4},{24,8},{28,12},{1,17},{... | collective-permute-start | bytes 4616 | tf_op jit(solution)/shard_map/ppermute | solution.py:100
  (70 other events, 386.4 us)

commit v2 on v1

v2 whole, which is shorter than its diff:
```python
import functools

import jax
import jax.numpy as jnp
from jax import lax
from jax.experimental import pallas as pl
from jax.experimental.pallas import tpu as pltpu
from jax.sharding import PartitionSpec as P

D = 768
HEADS = 12
HEAD_DIM = D // HEADS

EPS = 1e-06
NEG = -1e30
ROOT_HALF = 0.7071067811865476
INV_ROOT_TWO_PI = 0.3989422804014327
BF16 = jnp.bfloat16
F32 = jnp.float32
BLOCK_MOST = 256
EXTRA = 8
QTILE = 256
KTILE = 256


def matmul(left, right):
    return jnp.dot(left, right, preferred_element_type=F32)


def matmul_tn(left, right):
    return lax.dot_general(left, right, (((0,), (0,)), ((), ())), preferred_element_type=F32)


def matmul_nt(left, right):
    return lax.dot_general(left, right, (((1,), (1,)), ((), ())), preferred_element_type=F32)


def normalize(values):
    centre = values - jnp.mean(values, axis=-1, keepdims=True)
    inverse = lax.rsqrt(jnp.mean(centre * centre, axis=-1, keepdims=True) + EPS)
    return (centre * inverse, inverse)


def norm_back(upstream, normed, inverse, gain):
    shaped = upstream * gain
    centred = jnp.mean(shaped, axis=-1, keepdims=True)
    aligned = jnp.mean(shaped * normed, axis=-1, keepdims=True)
    return inverse * (shaped - centred - normed * aligned)


def pieces_of(column):
    high = column.astype(BF16).astype(F32)
    middle = (column - high).astype(BF16).astype(F32)
    return high, middle, column - high - middle


def with_pieces(base, lane, first, column):
    high, middle, low = pieces_of(column)
    base = jnp.where(lane == first, -high, base)
    base = jnp.where(lane == first + 1, -middle, base)
    return jnp.where(lane == first + 2, -low, base)


def lanes_of(head, rows):
    odd = lax.rem(head, 2)
    lane = lax.broadcasted_iota(jnp.int32, (rows, 2 * HEAD_DIM), 1)
    own = (lane >= HEAD_DIM * odd) & (lane < HEAD_DIM * (odd + 1))
    return odd, lane, own, HEAD_DIM * (1 - odd) + EXTRA


def nt(left, right):
    return lax.dot_general(left, right, (((1,), (1,)), ((), ())), preferred_element_type=F32)


def forward_kernel(
    reach, place_ref, tokens_ref, weights_ref, table_ref, marks_ref,
    context_ref, query_ref, key_ref, value_ref, query_s, key_s, value_s, context_s
):
    length = tokens_ref.shape[0]
    width = weights_ref.shape[1] // 3
    tiles = pl.cdiv(width, 128)
    depth = tokens_ref.shape[1]
    tokens = tokens_ref[...]
    bias = jnp.sum(weights_ref[depth:].astype(F32), axis=0, keepdims=True)
    for kind, (store, factor) in enumerate(
        ((query_s, HEAD_DIM**-0.5), (key_s, 1.0), (value_s, 1.0))
    ):
        columns = slice(kind * width, (kind + 1) * width)
        made = (nn(tokens, weights_ref[:depth, columns]) + bias[:, columns]) * factor
        for tile in range(tiles):
            last = min(128, width - 128 * tile)
            store[tile, :, :last] = made[:, 128 * tile : 128 * tile + last]

    def one_head(head, carry):
        tile = head // 2
        odd, lane, own, first = lanes_of(head, length)
        marks = marks_ref[odd].astype(F32)
        key_ref[head] = jnp.where(own, key_s[tile], marks).astype(BF16)
        ones = jnp.where((lane >= first) & (lane < first + 3), 1.0, 0.0)
        value_ref[head] = jnp.where(own, value_s[tile], ones).astype(BF16)
        odd, lane, own, first = lanes_of(head, QTILE)
        for start in range(0, length, QTILE):
            rows = slice(start, start + QTILE)
            seen = min(length, start + QTILE + reach)
            query = jnp.where(own, query_s[tile, rows], table_ref[odd, rows].astype(F32))
            scores = nt(query.astype(BF16), key_ref[head, :seen])
            highest = jnp.max(scores, axis=-1, keepdims=True)
            weights = jnp.exp(scores - highest).astype(BF16)
            mixed = nn(weights, value_ref[head, :seen])
            total = jnp.sum(jnp.where(lane == first, mixed, 0.0), axis=-1, keepdims=True)
            context_s[tile, rows] = jnp.where(own, mixed * (1.0 / total), context_s[tile, rows])
            query_ref[head, rows] = with_pieces(
                query, lane, first, highest + jnp.log(total)
            ).astype(BF16)
        return carry

    lax.fori_loop(0, width // HEAD_DIM, one_head, 0)
    for tile in range(tiles):
        last = min(128, width - 128 * tile)
        context_ref[:, 128 * tile : 128 * tile + last] = context_s[tile, :, :last].astype(BF16)


def nn(left, right):
    return jnp.dot(left, right, preferred_element_type=F32)


def tn(left, right):
    return lax.dot_general(left, right, (((0,), (0,)), ((), ())), preferred_element_type=F32)


def attend_forward(place, layer_in, weights, table, marks, length):
    width = weights.shape[1] // 3
    heads = width // HEAD_DIM
    tiles = pl.cdiv(width, 128)
    whole = pl.BlockSpec(memory_space=pltpu.VMEM)
    big = jax.ShapeDtypeStruct((heads, length, 128), BF16)
    return pl.pallas_call(
        functools.partial(forward_kernel, BLOCK_MOST),
        out_shape=(jax.ShapeDtypeStruct((length, width), BF16), big, big, big),
        grid_spec=pltpu.PrefetchScalarGridSpec(
            num_scalar_prefetch=1,
            grid=(1,),
            in_specs=[
                pl.BlockSpec((length, layer_in.shape[1]), lambda i, at: (at[0], 0)),
                whole,
                whole,
                whole,
            ],
            out_specs=(whole,) * 4,
            scratch_shapes=[pltpu.VMEM((tiles, length, 128), F32)] * 4,
        ),
        cost_estimate=pl.CostEstimate(
            flops=2 * length * D * 3 * width + 4 * length * length * 128 * heads,
            bytes_accessed=2 * (length * D + D * 3 * width + 4 * length * width),
            transcendentals=length * length * heads,
        ),
        name="attend_forward",
    )(place, layer_in, weights, table, marks)


def backward_kernel(
    reach, upstream_ref, out_ref, context_ref, query_ref, key_ref, value_ref,
    grads_ref, sums_ref, grad_s, context_s, query_s, query_t, key_s, value_s, extended_s
):
    length, width = context_ref.shape
    tiles = pl.cdiv(width, 128)
    made = nt(upstream_ref[...], out_ref[:width]).astype(BF16).astype(F32)
    context = context_ref[...].astype(F32)
    for tile in range(tiles):
        last = min(128, width - 128 * tile)
        grad_s[tile, :, :last] = made[:, 128 * tile : 128 * tile + last]
        context_s[tile, :, :last] = (made * context)[:, 128 * tile : 128 * tile + last]

    def one_head(head, carry):
        tile = head // 2
        odd, lane, own, first = lanes_of(head, length)
        centre = jnp.sum(jnp.where(own, context_s[tile], 0.0), axis=-1, keepdims=True)
        grad = jnp.where(own, grad_s[tile], 0.0)
        extended_s[...] = with_pieces(grad, lane, first, centre).astype(BF16)
        odd, lane, own, first = lanes_of(head, KTILE)
        query_s[...] = jnp.zeros_like(query_s)
        for start in range(0, length, KTILE):
            rows = slice(start, start + KTILE)
            seen = max(0, start - reach)
            scores = nt(key_ref[head, rows], query_ref[head, seen:])
            probs = jnp.exp(scores)
            pulled = nt(value_ref[head, rows], extended_s[seen:])
            changed = (probs * pulled).astype(BF16)
            grad_value = nn(probs.astype(BF16), extended_s[seen:])
            grad_key = nn(changed, query_ref[head, seen:])
            value_s[tile, rows] = jnp.where(own, grad_value, value_s[tile, rows])
            key_s[tile, rows] = jnp.where(own, grad_key, key_s[tile, rows])
            query_s[seen:] += tn(changed, key_ref[head, rows])
        odd, lane, own, first = lanes_of(head, length)
        query_t[tile] = jnp.where(own, query_s[...] * HEAD_DIM**-0.5, query_t[tile])
        return carry

    lax.fori_loop(0, width // HEAD_DIM, one_head, 0)
    for kind, store in enumerate((query_t, key_s, value_s)):
        for tile in range(tiles):
            last = min(128, width - 128 * tile)
            made = store[tile, :, :last]
            begin = kind * width + 128 * tile
            grads_ref[:, begin : begin + last] = made.astype(BF16)
            if kind != 1:
                sums_ref[kind : kind + 1, 128 * tile : 128 * tile + last] = jnp.sum(
                    made, axis=0, keepdims=True
                )


def attend_backward(upstream, out, saved):
    context, query, key, value = saved
    length, width = context.shape
    heads = width // HEAD_DIM
    tiles = pl.cdiv(width, 128)
    whole = pl.BlockSpec(memory_space=pltpu.VMEM)
    tall = pltpu.VMEM((tiles, length, 128), F32)
    return pl.pallas_call(
        functools.partial(backward_kernel, BLOCK_MOST),
        out_shape=(
            jax.ShapeDtypeStruct((length, 3 * width), BF16),
            jax.ShapeDtypeStruct((3, width), F32),
        ),
        in_specs=[whole] * 6,
        out_specs=(whole, whole),
        scratch_shapes=[
            tall, tall, pltpu.VMEM((length, 128), F32), tall, tall, tall,
            pltpu.VMEM((length, 128), BF16),
        ],
        cost_estimate=pl.CostEstimate(
            flops=2 * length * D * width + 10 * length * length * 128 * heads,
            bytes_accessed=2 * (length * D + 10 * length * width),
            transcendentals=length * length * heads,
        ),
        name="attend_backward",
    )(upstream, out, context, query, key, value)


def mask_terms(blocks, links):
    count = links.shape[0]
    numbers = lax.iota(jnp.int32, count)
    same_block = numbers[:, None] == numbers[None, :]
    earlier = (numbers[:, None] > numbers[None, :]) & (links == 1)
    table = jnp.where(same_block | earlier, 0.0, NEG).astype(BF16)
    onehot = (blocks[:, None] == numbers[None, :]).astype(BF16)
    seen = matmul(onehot, table).astype(BF16)
    ones = jnp.ones((blocks.shape[0], 3), BF16)
    marks = jnp.concatenate([onehot, ones], axis=1)

    def both(terms):
        after = ((0, 0), (HEAD_DIM, HEAD_DIM - terms.shape[1]))
        before = ((0, 0), (0, 2 * HEAD_DIM - terms.shape[1]))
        return jnp.stack([jnp.pad(terms, after), jnp.pad(terms, before)])

    return both(seen), both(marks)


def swap_tensor(array, mask):
    ways = lax.axis_size("tensor")
    return lax.ppermute(array, "tensor", [(i, i ^ mask) for i in range(ways)])


def swap_dp(array, mask):
    ways = lax.axis_size("dp")
    return lax.ppermute(array, "dp", [(i, i ^ mask) for i in range(ways)])


def across(array):
    return swap_tensor(array, 2)


def partner(array):
    return swap_tensor(array, 1)


def after(array, *earlier):
    return lax.optimization_barrier((array,) + earlier)[0]


def three_terms(row):
    high = lax.reduce_precision(row, 8, 7)
    middle = lax.reduce_precision(row - high, 8, 7)
    terms = jnp.stack([high, middle, row - high - middle]).astype(BF16)
    return jnp.pad(terms, ((0, 5), (0, 0)))


def scatter_pieces(pieces):
    return jnp.sum(lax.all_to_all(pieces, "dp", 0, 0).astype(F32), axis=0)


def by_rows(grad):
    ways = lax.axis_size("dp")
    return grad.reshape(ways, grad.shape[0] // ways, grad.shape[1])


def from_halves(first, second, swapped):
    return jnp.where(
        swapped,
        jnp.concatenate([second, first], axis=0),
        jnp.concatenate([first, second], axis=0),
    )


def on_device(
    layer_in,
    block_of,
    block_links,
    w_query,
    b_query,
    w_key,
    w_value,
    b_value,
    w_out,
    b_out,
    gain_one,
    shift_one,
    w_up,
    b_up,
    w_down,
    b_down,
    gain_two,
    shift_two,
    grad_out,
):
    length = block_of.shape[1]
    half = length // 2
    place = lax.axis_index("tensor")
    sequence = place // 2
    core = place % 2
    width = w_query.shape[1]
    rise_half = w_up.shape[0] // 2
    fall_half = w_down.shape[0] // 2

    bias_row = jnp.concatenate([b_query, jnp.zeros_like(b_query), b_value])
    qkv_mine = jnp.concatenate(
        [jnp.concatenate([w_query, w_key, w_value], axis=1), three_terms(bias_row)], axis=0
    )
    out_mine = jnp.concatenate([w_out, three_terms(b_up)], axis=0)
    odd = lax.axis_index("dp") % 2
    qkv_other = across(qkv_mine)
    up_first = across(lax.dynamic_slice_in_dim(w_up, odd * rise_half, rise_half, 0))
    out_other = across(out_mine)
    down_first = across(lax.dynamic_slice_in_dim(w_down, odd * fall_half, fall_half, 0))

    tokens = lax.dynamic_slice_in_dim(layer_in, sequence * length, length, 0)
    tokens_mine = lax.dynamic_slice_in_dim(tokens, core * half, half, 0).astype(F32)
    blocks = lax.dynamic_index_in_dim(block_of, sequence, 0, keepdims=False)
    links = lax.dynamic_index_in_dim(block_links, sequence, 0, keepdims=False)
    table, marks = mask_terms(blocks, links)
    chosen = jnp.full((1,), sequence, jnp.int32)

    saved_mine = attend_forward(chosen, layer_in, qkv_mine, table, marks, length)
    saved_other = attend_forward(chosen, layer_in, qkv_other, table, marks, length)
    context_mine = saved_mine[0]
    context_other = after(saved_other[0], up_first)
    up_second = swap_dp(up_first, 1)
    context = jnp.concatenate([context_mine, context_other], axis=1)
    out_both = jnp.concatenate([w_out, out_other[:width]], axis=0)
    b_up_other = jnp.sum(out_other[width:].astype(F32), axis=0)

    far = lax.dynamic_slice_in_dim(context, (1 - core) * half, half, 0)
    near = lax.dynamic_slice_in_dim(context, core * half, half, 0)
    branch = matmul(near, out_both) + partner(matmul(far, out_both).astype(BF16)).astype(F32)
    normed_one, inverse_one = normalize(tokens_mine + branch + b_out)
    hidden_one = normed_one * gain_one + shift_one
    hidden_low_mine = after(hidden_one.astype(BF16), down_first)
    down_second = swap_dp(down_first, 1)
    hidden_low = jnp.concatenate([hidden_low_mine, partner(hidden_low_mine)], axis=0)

    def rise(weights, bias):
        up = matmul(hidden_low, weights) + bias
        phi = 0.5 * (1.0 + lax.erf(up * ROOT_HALF))
        slope = phi + up * INV_ROOT_TWO_PI * jnp.exp(-0.5 * up * up)
        return (up * phi).astype(BF16), slope

    active_mine, slope_mine = rise(w_up, b_up)
    up_other = from_halves(up_first, up_second, odd == 1)
    active_other, slope_other = rise(up_other, b_up_other)
    down_other = from_halves(down_first, down_second, odd == 1)
    ffn_terms = matmul(active_mine, w_down) + matmul(active_other, down_other)
    ffn = ffn_terms[:half] + partner(ffn_terms[half:].astype(BF16)).astype(F32)
    normed_two, inverse_two = normalize(hidden_one + ffn + b_down)
    layer_out = (normed_two * gain_two + shift_two).astype(BF16)

    upstream = grad_out.astype(F32)
    grad_gain_two = jnp.sum(upstream * normed_two, axis=0)
    grad_shift_two = jnp.sum(upstream, axis=0)
    grad_two = norm_back(upstream, normed_two, inverse_two, gain_two)
    grad_b_down = jnp.sum(grad_two, axis=0)
    ffn_grad_mine = grad_two.astype(BF16)
    ffn_grad = jnp.concatenate([ffn_grad_mine, partner(ffn_grad_mine)], axis=0)

    down_received = across(matmul_tn(ffn_grad, active_other).astype(BF16))
    grad_up_other = matmul_nt(ffn_grad, down_other) * slope_other
    up_low_other = grad_up_other.astype(BF16)
    up_received = across(matmul_tn(hidden_low, up_low_other).astype(BF16))
    grad_up_mine = matmul_nt(ffn_grad, w_down) * slope_mine
    up_low_mine = grad_up_mine.astype(BF16)
    hidden_terms = matmul_nt(up_low_mine, w_up) + matmul_nt(up_low_other, up_other)
    grad_hidden = grad_two + hidden_terms[:half] + partner(
        hidden_terms[half:].astype(BF16)
    ).astype(F32)
    down_mine = matmul_tn(ffn_grad, active_mine)
    up_mine = matmul_tn(hidden_low, up_low_mine)

    grad_gain_one = jnp.sum(grad_hidden * normed_one, axis=0)
    grad_shift_one = jnp.sum(grad_hidden, axis=0)
    grad_one = norm_back(grad_hidden, normed_one, inverse_one, gain_one)
    grad_b_out = jnp.sum(grad_one, axis=0)
    one_low = grad_one.astype(BF16)
    one_partner = partner(one_low)
    pair = jnp.concatenate([one_low, one_partner, one_low], axis=0)
    branch_grad = lax.dynamic_slice_in_dim(pair, core * half, length, 0)

    out_received = across(matmul_tn(branch_grad, context_other).astype(BF16))

    row_sums = jnp.stack(
        [grad_b_out, grad_gain_one, grad_shift_one, grad_b_down, grad_gain_two, grad_shift_two]
    )
    row_sums = row_sums + partner(row_sums)
    hidden_mine = jnp.sum(grad_up_mine, axis=0).reshape(-1, D)
    hidden_other = jnp.sum(grad_up_other, axis=0).reshape(-1, D)
    sums = jnp.concatenate([row_sums, hidden_mine], axis=0) + across(
        jnp.concatenate([row_sums, hidden_other], axis=0)
    )
    sum_high = lax.reduce_precision(sums, 8, 7)
    sum_terms = jnp.concatenate([sum_high, sums - sum_high], axis=0).astype(BF16)

    low_other, columns_other = attend_backward(branch_grad, out_other, saved_other)
    low_mine, columns_mine = attend_backward(
        after(branch_grad, low_other, sums), out_mine, saved_mine
    )

    down_received = after(down_received, low_other)
    down_pieces = by_rows((down_mine + down_received.astype(F32)).astype(BF16))
    ways, share = down_pieces.shape[:2]
    count = sum_terms.shape[0]
    sum_pieces = jnp.broadcast_to(
        jnp.pad(sum_terms, ((0, -count % 8), (0, 0)))[None], (ways, count + -count % 8, D)
    )
    down_sums = scatter_pieces(jnp.concatenate([down_pieces, sum_pieces], axis=1))
    grad_w_down = down_sums[:share].T
    sums = jnp.sum(down_sums[share : share + count].reshape(2, count // 2, D), axis=0)

    def with_bias(columns):
        row = jnp.concatenate([columns[0], jnp.zeros_like(columns[0]), columns[2]])
        return row, three_terms(row)

    other_row, other_terms = with_bias(columns_other)
    qkv_received = across(
        jnp.concatenate([matmul_tn(tokens, low_other).astype(BF16), other_terms], axis=0)
    )

    up_received, out_received = (
        lax.optimization_barrier((up_received, out_received, low_mine))[:2]
    )
    up_sum = (up_mine + up_received.astype(F32)).astype(BF16)
    out_sum = matmul_tn(branch_grad, context_mine) + out_received.astype(F32)
    up_pieces = jnp.concatenate([by_rows(up_sum), by_rows(out_sum.astype(BF16))], axis=2)
    up_out = scatter_pieces(up_pieces)
    grad_w_up, grad_w_out = up_out[:, : w_up.shape[1]], up_out[:, w_up.shape[1] :].T

    mine_row, _ = with_bias(columns_mine)
    qkv_received = qkv_received.astype(F32)
    qkv_sum = matmul_tn(tokens, low_mine) + qkv_received[:D]
    bias_terms = three_terms(mine_row + jnp.sum(qkv_received[D:], axis=0))
    qkv_pieces = by_rows(qkv_sum.astype(BF16))
    bias_pieces = jnp.broadcast_to(bias_terms[None], (ways,) + bias_terms.shape)
    qkv = scatter_pieces(jnp.concatenate([qkv_pieces, bias_pieces], axis=1))
    bias_sums = jnp.sum(qkv[share:], axis=0)
    qkv = qkv[:share]

    in_terms = matmul_nt(low_mine, qkv_mine[:D]) + matmul_nt(low_other, qkv_other[:D])
    in_far = lax.dynamic_slice_in_dim(in_terms, (1 - core) * half, half, 0)
    in_near = lax.dynamic_slice_in_dim(in_terms, core * half, half, 0)
    grad_in = grad_one + in_near + partner(in_far.astype(BF16)).astype(F32)

    return (
        layer_out,
        grad_in,
        qkv[:, :width],
        bias_sums[:width],
        qkv[:, width : 2 * width],
        qkv[:, 2 * width :],
        bias_sums[2 * width :],
        grad_w_out,
        sums[0],
        sums[1],
        sums[2],
        grad_w_up,
        sums[6:].reshape(-1),
        grad_w_down,
        sums[3],
        sums[4],
        sums[5],
    )


def solution(mesh):
    in_specs = (
        P("dp", None),
        P("dp", None),
        P("dp", None, None),
        P(None, "tensor"),
        P("tensor"),
        P(None, "tensor"),
        P(None, "tensor"),
        P("tensor"),
        P("tensor", None),
        P(),
        P(),
        P(),
        P(None, "tensor"),
        P("tensor"),
        P("tensor", None),
        P(),
        P(),
        P(),
        P(("dp", "tensor"), None),
    )
    out_specs = (
        P(("dp", "tensor"), None),
        P(("dp", "tensor"), None),
        P("dp", "tensor"),
        P("tensor"),
        P("dp", "tensor"),
        P("dp", "tensor"),
        P("tensor"),
        P("tensor", "dp"),
        P(),
        P(),
        P(),
        P("dp", "tensor"),
        P("tensor"),
        P("tensor", "dp"),
        P(),
        P(),
        P(),
    )
    return jax.shard_map(
        on_device, mesh=mesh, in_specs=in_specs, out_specs=out_specs, check_vma=False
    )
```

time: 329 us -> 315 us (0.957)
  Pallas kernels: 0 us -> 48.4 us
  matrix products: 97.9 us -> 72.6 us
  other arithmetic: 39.7 us -> 20.8 us
  starting transfers between devices: 40.9 us -> 32 us
  local copies, waits for them, and re-layouts: 25.4 us -> 20.4 us
    pallas_call x0 -> x4, Pallas kernels: none -> 48.4 us  [the longest x2 25.5 us: attend_backward(): pl.pallas_call(functools.partial(backward_kernel, BLOCK_MOST), out_shape=...]
    dot_general x12 -> x0, matrix products: 41.6 us -> none  [the longest x2 10.5 us: attend_backward(): pulled = jnp.einsum('qhd,khd->hqk', grad, value, preferred_element_type=F32)]
    all_to_all x3, waiting for transfers between devices: 1.45 us -> 27.7 us  [scatter_pieces(): return jnp.sum(lax.all_to_all(pieces, 'dp', 0, 0).astype(F32), axis=0)]
    ppermute x20 -> x17, waiting for transfers between devices: 100 us -> 82.3 us  [swap_tensor(): return lax.ppermute(array, 'tensor', [(i, i ^ mask) for i in range(ways)])]
    dot_general x8 -> x7, matrix products: 14.2 us -> 30.7 us  [matmul(): return jnp.dot(left, right, preferred_element_type=F32)]
    convert_element_type x5 -> x2, other arithmetic: 15.7 us -> 0.45 us  [the longest x1 0.31 us: on_device(): hidden_low_mine = after(hidden_one.astype(BF16), down_first)]
    ppermute x6 -> x2, waiting for transfers between devices: 18.2 us -> 7.68 us  [swap_dp(): return lax.ppermute(array, 'dp', [(i, i ^ mask) for i in range(ways)])]
    ppermute x6 -> x2, starting transfers between devices: 9.94 us -> 2.09 us  [swap_dp(): return lax.ppermute(array, 'dp', [(i, i ^ mask) for i in range(ways)])]
  transfers between devices with their start and end apart: 29 -> 22, of which waited for: 13 -> 13; matrix products, arithmetic and copies ran while one was open for 38% -> 24% of each run, Pallas kernels for 0% -> 15%
where the time goes in v2:
time: 315 us; the launch traced here: 314 us
  waiting for transfers between devices  118 us (37%)
  matrix products  72.6 us (23%)
  Pallas kernels  48.4 us (15%)
  starting transfers between devices  32 us (10%)
  other arithmetic  20.8 us (7%)
  local copies, waits for them, and re-layouts  20.4 us (6%)
    ppermute x17, waiting for transfers between devices, swap_tensor(): return lax.ppermute(array, 'tensor', [(i, i ^ mask) for i in range(ways)])  82.3 us
    dot_general x7, matrix products, matmul(): return jnp.dot(left, right, preferred_element_type=F32)  30.7 us
    all_to_all x3, waiting for transfers between devices, scatter_pieces(): return jnp.sum(lax.all_to_all(pieces, 'dp', 0, 0).astype(F32), axis=0)  27.7 us
    pallas_call x2, Pallas kernels, attend_backward(): pl.pallas_call(functools.partial(backward_kernel, BLOCK_MOST), out_shape=...  25.5 us
    pallas_call x2, Pallas kernels, attend_forward(): pl.pallas_call(functools.partial(forward_kernel, BLOCK_MOST), out_shape=(...  22.9 us
    dot_general x8, matrix products, matmul_tn(): lax.dot_general(left, right, (((0,), (0,)), ((), ())), preferred_element_...  22.7 us
    dot_general x6, matrix products, matmul_nt(): lax.dot_general(left, right, (((1,), (1,)), ((), ())), preferred_element_...  19.2 us
    all_to_all x3, starting transfers between devices, scatter_pieces(): return jnp.sum(lax.all_to_all(pieces, 'dp', 0, 0).astype(F32), axis=0)  16.1 us
  transfers between devices with their start and end apart: 22, of which 13 were waited for; matrix products, arithmetic and copies ran while one was open for 24% of the time, Pallas kernels for 15%

profile of v2, /device:TPU:0, one launch (start us, length us, event | category | flops | bytes accessed | tf_op | source)
XLA Modules:
  0.0 313.8 jit_solution(16000143343403013429)
XLA Ops:
  4.6 3.0 collective-permute-start
  13.7 11.5 %attend_forward.2 = (bf16[1024,192]{1,0:T(8,128)(2,1)}, bf16[3,1024,128]{2,1,0:T(8,128)(2,1)}, bf16[3,1024,128]{2,1,0:T(8,128)(2,1)}, bf16[3,1024,128]{2,1,0:T(8,128)(2,1)}) custom-call(s32[1]{0:T(128)} %bitcast.place_ref, bf16[2048,768]{1,0:T(8,128)(2,1)} %tokens_ref.3, bf16[776,576]{1,0:T(8,128)(2,1)} %copy-done.17, ...), custom_call_target="tpu_custom_call" | custom-call | flops 2516582400 | bytes 4030464 | tf_op jit(solution)/shard_map/attend_forward/pallas_call | solution.py:137
  25.2 23.6 %collective-permute-done.2.out_ref = bf16[200,768]{1,0:T(8,128)(2,1)S(1)} collective-permute-done((bf16[200,768]{1,0:T(8,128)(2,1)S(1)}, bf16[200,768]{1,0:T(8,128)(2,1)S(1)}, u32[]{:S(2)}, u32[]{:S(2)}) %collective-permute-start.2) | collective-permute-done | bytes 307232 | tf_op jit(solution)/shard_map/ppermute | solution.py:260
  48.9 11.4 %attend_forward.3 = (bf16[1024,192]{1,0:T(8,128)(2,1)}, bf16[3,1024,128]{2,1,0:T(8,128)(2,1)}, bf16[3,1024,128]{2,1,0:T(8,128)(2,1)}, bf16[3,1024,128]{2,1,0:T(8,128)(2,1)}) custom-call(s32[1]{0:T(128)} %bitcast.place_ref, bf16[2048,768]{1,0:T(8,128)(2,1)} %tokens_ref.3, bf16[776,576]{1,0:T(8,128)(2,1)} %collective-permute-done.weights_ref, ...), custom_call_target="tpu_custom_call" | custom-call | flops 2516582400 | bytes 4030464 | tf_op jit(solution)/shard_map/attend_forward/pallas_call | solution.py:137
  69.1 10.8 %collective-permute-done.4 = bf16[384,768]{1,0:T(8,128)(2,1)} collective-permute-done((bf16[384,768]{1,0:T(8,128)(2,1)}, bf16[384,768]{1,0:T(8,128)(2,1)}, u32[]{:S(2)}, u32[]{:S(2)}) %collective-permute-start.4) | collective-permute-done | bytes 589856 | tf_op jit(solution)/shard_map/ppermute | solution.py:260
  84.0 4.0 %multiply_convert_fusion.1 = (bf16[1024,768]{1,0:T(8,128)(2,1)S(1)}, f32[1024,768]{1,0:T(8,128)S(1)}) fusion(f32[768]{0:T(1024)S(1)} %copy-done.35, bf16[1024,768]{1,0:T(8,128)(2,1)S(1)} %constant_dynamic-update-slice_fusion, bf16[768,768]{1,0:T(8,128)(2,1)S(1)} %copy-done), kind=kOutput, calls=%fused_computation.13 | convolution fusion | flops 1212678144 | bytes 7474176 | tf_op jit(solution)/shard_map/dot_general | solution.py:27
  89.4 7.7 %collective-permute-done.6 = bf16[384,768]{1,0:T(8,128)(2,1)S(1)} collective-permute-done((bf16[384,768]{1,0:T(8,128)(2,1)}, bf16[384,768]{1,0:T(8,128)(2,1)S(1)}, u32[]{:S(2)}, u32[]{:S(2)}) %collective-permute-start.6) | collective-permute-done | bytes 589856 | tf_op jit(solution)/shard_map/ppermute | solution.py:265
  97.1 16.7 %multiply_convert_fusion = (bf16[1024,768]{1,0:T(8,128)(2,1)S(1)}, f32[1024,768]{1,0:T(8,128)S(1)}) fusion(f32[768]{0:T(1024)S(1)} %convert_reduce_fusion.4, bf16[1024,768]{1,0:T(8,128)(2,1)S(1)} %constant_dynamic-update-slice_fusion, bf16[384,768]{1,0:T(8,128)(2,1)} %collective-permute-done.1, bf16[384,768]{1,0:T(8,128)(2,1)S(1)} %collective-permute-done.6, ...), kind=kOutput, calls=%fused_computation.11 | convolution fusion | flops 1217986560 | bytes 7474177 | tf_op jit(solution)/shard_map/dot_general | solution.py:27
  113.8 3.3 %convolution_add_fusion.2 = f32[1024,768]{1,0:T(8,128)S(1)} fusion(f32[1024,768]{1,0:T(8,128)S(1)} %fusion.103, bf16[1024,768]{1,0:T(8,128)(2,1)S(1)} %get-tuple-element.161, bf16[384,768]{1,0:T(8,128)(2,1)} %collective-permute-done.4, bf16[384,768]{1,0:T(8,128)(2,1)S(1)} %collective-permute-done.7, pred[]{:T(512)S(6)} %eq.60), kind=kOutput, calls=%fused_computation.34 | convolution fusion | flops 1214054400 | bytes 9043969 | tf_op jit(solution)/shard_map/dot_general | solution.py:27
  126.2 3.8 %fusion.102 = (f32[768]{0:T(1024)}, bf16[1024,768]{1,0:T(8,128)(2,1)S(1)}) fusion(f32[1024,768]{1,0:T(8,128)S(1)} %get-tuple-element.160, f32[768]{0:T(1024)S(1)} %copy-done.35, bf16[768,768]{1,0:T(8,128)(2,1)S(1)} %copy-done.23, bf16[512,768]{1,0:T(8,128)(2,1)S(1)} %collective-permute-done.9, bf16[512,768]{1,0:T(8,128)(2,1)S(1)} %convert_element_type.138), kind=kOutput, calls=%fused_computation.218 | convolution fusion | flops 1220541696 | bytes 7477248 | tf_op jit(solution)/shard_map/dot_general | solution.py:35
  131.5 3.5 %fusion.101 = (f32[768]{0:T(1024)S(1)}, bf16[1024,768]{1,0:T(8,128)(2,1)S(1)}) fusion(f32[1024,768]{1,0:T(8,128)S(1)} %get-tuple-element.162, f32[768]{0:T(1024)S(1)} %convert_reduce_fusion.4, bf16[384,768]{1,0:T(8,128)(2,1)} %collective-permute-done.4, bf16[384,768]{1,0:T(8,128)(2,1)S(1)} %collective-permute-done.7, pred[]{:T(512)S(6)} %eq.60, ...), kind=kOutput, calls=%fused_computation.217 | convolution fusion | flops 1225850112 | bytes 7477249 | tf_op jit(solution)/shard_map/dot_general | solution.py:35
  135.0 3.3 %convolution_add_fusion.1 = f32[1024,768]{1,0:T(8,128)S(1)} fusion(f32[1024,768]{1,0:T(8,128)S(1)} %fusion.40, bf16[1024,768]{1,0:T(8,128)(2,1)S(1)} %get-tuple-element.164, bf16[384,768]{1,0:T(8,128)(2,1)} %collective-permute-done.1, bf16[384,768]{1,0:T(8,128)(2,1)S(1)} %collective-permute-done.6, pred[]{:T(512)S(6)} %eq.60), kind=kOutput, calls=%fused_computation.33 | convolution fusion | flops 1214054400 | bytes 9043969 | tf_op jit(solution)/shard_map/dot_general | solution.py:35
  144.1 3.9 %convolution_convert_fusion = bf16[768,768]{1,0:T(8,128)(2,1)} fusion(bf16[1024,768]{1,0:T(8,128)(2,1)} %copy-done.48, bf16[512,768]{1,0:T(8,128)(2,1)S(1)} %copy-done.41, bf16[512,768]{1,0:T(8,128)(2,1)S(1)} %convert_element_type.138), kind=kOutput, calls=%fused_computation.60 | convolution fusion | flops 1211695104 | bytes 4325376 | tf_op jit(solution)/shard_map/dot_general | solution.py:31
  150.1 26.6 %collective-permute-done.13 = f32[7,768]{1,0:T(8,128)S(1)} collective-permute-done((f32[7,768]{1,0:T(8,128)S(1)}, f32[7,768]{1,0:T(8,128)S(1)}, u32[]{:S(2)}, u32[]{:S(2)}) %collective-permute-start.13) | collective-permute-done | bytes 21536 | tf_op jit(solution)/shard_map/ppermute | solution.py:260
  176.8 3.9 %fusion.17.upstream_ref = bf16[1024,768]{1,0:T(8,128)(2,1)} fusion(s32[]{:T(128)S(6)} %select_n.74, bf16[512,768]{1,0:T(8,128)(2,1)S(1)} %convert_element_type.142, bf16[512,768]{1,0:T(8,128)(2,1)S(1)} %collective-permute-done.11), kind=kLoop, calls=%fused_computation.39 | loop fusion | flops 4718592 | bytes 3145732 | tf_op jit(solution)/shard_map/concatenate | solution.py:412
  180.7 13.0 %attend_backward.2 = (bf16[1024,576]{1,0:T(8,128)(2,1)}, f32[3,192]{1,0:T(4,128)}) custom-call(bf16[1024,768]{1,0:T(8,128)(2,1)} %fusion.17.upstream_ref, bf16[200,768]{1,0:T(8,128)(2,1)} %copy-done.20, bf16[1024,192]{1,0:T(8,128)(2,1)} %get-tuple-element.37.context_ref, bf16[3,1024,128]{2,1,0:T(8,128)(2,1)} %get-tuple-element.39.query_ref, ...), custom_call_target="tpu_custom_call" | custom-call | flops 4328521728 | bytes 5505024 | tf_op jit(solution)/shard_map/attend_backward/pallas_call | solution.py:218
  193.7 3.2 %add_convert_fusion = bf16[768,768]{1,0:T(8,128)(2,1)S(1)} fusion(bf16[768,768]{1,0:T(8,128)(2,1)} %collective-permute-done.18, bf16[1024,768]{1,0:T(8,128)(2,1)} %copy-done.51, bf16[512,768]{1,0:T(8,128)(2,1)S(1)} %copy-done.42, bf16[512,768]{1,0:T(8,128)(2,1)S(1)} %convert_element_type.138), kind=kOutput, calls=%fused_computation.22 | convolution fusion | flops 1212874752 | bytes 5505024 | tf_op jit(solution)/shard_map/dot_general | solution.py:31
  198.0 6.2 %all-to-all-start.2 = ((bf16[8,112,768]{2,1,0:T(8,128)(2,1)}), bf16[8,112,768]{2,1,0:T(8,128)(2,1)S(1)}, u32[]{:S(2)}, u32[]{:S(2)}) async-start(bf16[8,112,768]{2,1,0:T(8,128)(2,1)} %pad_maximum_fusion.2), calls=%async_computation.2 | async-start | bytes 2752512 | tf_op jit(solution)/shard_map/all_to_all | solution.py:288
  204.5 2.9 convolution_convert_fusion.2
  210.1 4.3 %convolution_convert_fusion.1 = bf16[768,768]{1,0:T(8,128)(2,1)} fusion(bf16[1024,768]{1,0:T(8,128)(2,1)} %copy-done.18, bf16[1024,768]{1,0:T(8,128)(2,1)} %copy-done.47), kind=kOutput, calls=%fused_computation.61 | convolution fusion | flops 1208549376 | bytes 4325376 | tf_op jit(solution)/shard_map/dot_general | solution.py:31
  214.9 12.5 %attend_backward.3 = (bf16[1024,576]{1,0:T(8,128)(2,1)}, f32[3,192]{1,0:T(4,128)}) custom-call(bf16[1024,768]{1,0:T(8,128)(2,1)} %fusion.17.upstream_ref, bf16[200,768]{1,0:T(8,128)(2,1)} %copy-done.21, bf16[1024,192]{1,0:T(8,128)(2,1)} %get-tuple-element.35.context_ref, bf16[3,1024,128]{2,1,0:T(8,128)(2,1)} %get-tuple-element.44.query_ref, ...), custom_call_target="tpu_custom_call" | custom-call | flops 4328521728 | bytes 5505024 | tf_op jit(solution)/shard_map/attend_backward/pallas_call | solution.py:218
  228.2 5.3 %collective-permute-done.15 = bf16[776,576]{1,0:T(8,128)(2,1)} collective-permute-done((bf16[776,576]{1,0:T(8,128)(2,1)S(1)}, bf16[776,576]{1,0:T(8,128)(2,1)}, u32[]{:S(2)}, u32[]{:S(2)}) %collective-permute-start.15) | collective-permute-done | bytes 893984 | tf_op jit(solution)/shard_map/ppermute | solution.py:260
  237.3 2.6 fusion.12
  242.9 6.3 %all-to-all-start = ((bf16[8,104,576]{2,1,0:T(8,128)(2,1)}), bf16[8,104,576]{2,1,0:T(8,128)(2,1)S(1)}, u32[]{:S(2)}, u32[]{:S(2)}) async-start(bf16[8,104,576]{2,1,0:T(8,128)(2,1)} %pad_maximum_fusion.3), calls=%async_computation | async-start | bytes 2129920 | tf_op jit(solution)/shard_map/all_to_all | solution.py:288
  252.9 3.2 %fusion.31 = f32[1024,768]{1,0:T(8,128)} fusion(bf16[1024,576]{1,0:T(8,128)(2,1)S(1)} %copy-done.50, bf16[768,192]{1,0:T(8,128)(2,1)S(1)} %copy-done.16, bf16[768,192]{1,0:T(8,128)(2,1)S(1)} %copy-done.14, bf16[768,192]{1,0:T(8,128)(2,1)S(1)} %copy-done.12), kind=kOutput, calls=%fused_computation.82 | convolution fusion | flops 908623872 | bytes 5210112 | tf_op jit(solution)/shard_map/dot_general | solution.py:35
  256.1 2.7 collective-permute-done.16
  258.8 4.3 %collective-permute-done.17 = bf16[768,192]{0,1:T(8,128)(2,1)S(1)} collective-permute-done((bf16[768,192]{0,1:T(8,128)(2,1)S(1)}, bf16[768,192]{0,1:T(8,128)(2,1)S(1)}, u32[]{:S(2)}, u32[]{:S(2)}) %collective-permute-start.17) | collective-permute-done | bytes 294944 | tf_op jit(solution)/shard_map/ppermute | solution.py:260
  263.9 3.2 %add_convert_fusion.1 = bf16[768,768]{1,0:T(8,128)(2,1)S(1)} fusion(bf16[768,768]{1,0:T(8,128)(2,1)} %collective-permute-done.16, bf16[1024,768]{1,0:T(8,128)(2,1)S(1)} %copy-done.19, bf16[1024,768]{1,0:T(8,128)(2,1)} %copy-done.52), kind=kOutput, calls=%fused_computation.23 | convolution fusion | flops 1209729024 | bytes 5505024 | tf_op jit(solution)/shard_map/dot_general | solution.py:31
  268.5 3.0 all-to-all-done
  272.5 3.6 %all-to-all-start.1 = ((bf16[8,96,960]{2,1,0:T(8,128)(2,1)}), bf16[8,96,960]{2,1,0:T(8,128)(2,1)S(1)}, u32[]{:S(2)}, u32[]{:S(2)}) async-start(bf16[8,96,960]{2,1,0:T(8,128)(2,1)} %pad_maximum_fusion.1), calls=%async_computation.1 | async-start | bytes 3145728 | tf_op jit(solution)/shard_map/all_to_all | solution.py:288
  276.1 4.0 %convolution_add_fusion = f32[1024,768]{1,0:T(8,128)S(1)} fusion(f32[1024,768]{1,0:T(8,128)} %fusion.31, bf16[1024,576]{1,0:T(8,128)(2,1)} %get-tuple-element.42, bf16[776,576]{1,0:T(8,128)(2,1)} %collective-permute-done.weights_ref), kind=kOutput, calls=%fused_computation.30 | convolution fusion | flops 906756096 | bytes 8585216 | tf_op jit(solution)/shard_map/dot_general | solution.py:35
  287.1 24.8 %all-to-all-done.1 = bf16[8,96,960]{2,1,0:T(8,128)(2,1)S(1)} async-done(((bf16[8,96,960]{2,1,0:T(8,128)(2,1)}), bf16[8,96,960]{2,1,0:T(8,128)(2,1)S(1)}, u32[]{:S(2)}, u32[]{:S(2)}) %all-to-all-start.1) | async-done | bytes 1474592 | tf_op jit(solution)/shard_map/all_to_all | solution.py:288
  (242 shorter events, 69.8 us)
Async XLA Ops:
  4.6 44.3 %collective-permute-start = (bf16[776,576]{1,0:T(8,128)(2,1)S(1)}, bf16[776,576]{1,0:T(8,128)(2,1)}, u32[]{:S(2)}, u32[]{:S(2)}) collective-permute-start(bf16[776,576]{1,0:T(8,128)(2,1)S(1)} %pad_maximum_fusion.4.weights_ref), channel_id=1, source_target_pairs={{0,2},{1,3},{2,0},{3,1},{4,6},{5,7},{6,4},{7,5},{8,10},{9,11},{10,... | collective-permute-start | bytes 2681864 | tf_op jit(solution)/shard_map/ppermute | solution.py:260
  8.5 51.8 %collective-permute-start.1 = (bf16[384,768]{1,0:T(8,128)(2,1)}, bf16[384,768]{1,0:T(8,128)(2,1)}, u32[]{:S(2)}, u32[]{:S(2)}) collective-permute-start(bf16[384,768]{1,0:T(8,128)(2,1)} %constant_dynamic-slice_fusion.1), channel_id=1, source_target_pairs={{0,2},{1,3},{2,0},{3,1},{4,6},{5,7},{6,4},{7,5},{8,10},{9,11},{10,... | collective-permute-start | bytes 1769480 | tf_op jit(solution)/shard_map/ppermute | solution.py:260
  9.9 39.0 %collective-permute-start.2 = (bf16[200,768]{1,0:T(8,128)(2,1)S(1)}, bf16[200,768]{1,0:T(8,128)(2,1)S(1)}, u32[]{:S(2)}, u32[]{:S(2)}) collective-permute-start(bf16[200,768]{1,0:T(8,128)(2,1)S(1)} %pad_maximum_fusion.10.out_ref), channel_id=1, source_target_pairs={{0,2},{1,3},{2,0},{3,1},{4,6},{5,7},{6,4},{7,5},{8,10},{9,11},{10,... | collective-permute-start | bytes 921608 | tf_op jit(solution)/shard_map/ppermute | solution.py:260
  48.8 11.5 %copy-start.20 = (bf16[200,768]{1,0:T(8,128)(2,1)}, bf16[200,768]{1,0:T(8,128)(2,1)S(1)}, u32[]{:S(2)}) copy-start(bf16[200,768]{1,0:T(8,128)(2,1)S(1)} %collective-permute-done.2.out_ref) | copy-start | bytes 921604
  48.9 11.5 %copy-start.26 = (bf16[192,768]{1,0:T(8,128)(2,1)}, bf16[192,768]{1,0:T(8,128)(2,1)S(1)}, u32[]{:S(2)}) copy-start(bf16[192,768]{1,0:T(8,128)(2,1)S(1)} %slice.126) | copy-start | bytes 884740
  48.9 11.5 %copy-start.24 = (bf16[192,768]{1,0:T(8,128)(2,1)S(1)}, bf16[192,768]{1,0:T(8,128)(2,1)}, u32[]{:S(2)}) copy-start(bf16[192,768]{1,0:T(8,128)(2,1)} %param.27) | copy-start | bytes 884740
  48.9 11.4 %copy-start.44 = (bf16[1024,192]{1,0:T(8,128)(2,1)S(1)}, bf16[1024,192]{1,0:T(8,128)(2,1)}, u32[]{:S(2)}) copy-start(bf16[1024,192]{1,0:T(8,128)(2,1)} %get-tuple-element.35.context_ref) | copy-start | bytes 1179652
  62.9 2.6 collective-permute-start.3
  63.8 16.1 %collective-permute-start.4 = (bf16[384,768]{1,0:T(8,128)(2,1)}, bf16[384,768]{1,0:T(8,128)(2,1)}, u32[]{:S(2)}, u32[]{:S(2)}) collective-permute-start(bf16[384,768]{1,0:T(8,128)(2,1)} %constant_dynamic-slice_fusion), channel_id=1, source_target_pairs={{0,2},{1,3},{2,0},{3,1},{4,6},{5,7},{6,4},{7,5},{8,10},{9,11},{10,... | collective-permute-start | bytes 1769480 | tf_op jit(solution)/shard_map/ppermute | solution.py:260
  79.9 2.9 collective-permute-start.5
  80.6 16.5 %collective-permute-start.6 = (bf16[384,768]{1,0:T(8,128)(2,1)}, bf16[384,768]{1,0:T(8,128)(2,1)S(1)}, u32[]{:S(2)}, u32[]{:S(2)}) collective-permute-start(bf16[384,768]{1,0:T(8,128)(2,1)} %collective-permute-done.1), channel_id=1, source_target_pairs={{0,4},{4,0},{8,12},{12,8},{16,20},{20,16},{24,28},{28,24},{1,5},{5... | collective-permute-start | bytes 1769480 | tf_op jit(solution)/shard_map/ppermute | solution.py:265
  82.4 31.4 %collective-permute-start.7 = (bf16[384,768]{1,0:T(8,128)(2,1)}, bf16[384,768]{1,0:T(8,128)(2,1)S(1)}, u32[]{:S(2)}, u32[]{:S(2)}) collective-permute-start(bf16[384,768]{1,0:T(8,128)(2,1)} %collective-permute-done.4), channel_id=1, source_target_pairs={{0,4},{4,0},{8,12},{12,8},{16,20},{20,16},{24,28},{28,24},{1,5},{5... | collective-permute-start | bytes 1769480 | tf_op jit(solution)/shard_map/ppermute | solution.py:265
  84.0 13.1 %copy-start.18 = (bf16[1024,768]{1,0:T(8,128)(2,1)}, bf16[1024,768]{1,0:T(8,128)(2,1)S(1)}, u32[]{:S(2)}) copy-start(bf16[1024,768]{1,0:T(8,128)(2,1)S(1)} %constant_dynamic-update-slice_fusion) | copy-start | bytes 4718596
  117.2 2.4 collective-permute-start.8
  123.9 2.4 collective-permute-start.9
  138.4 2.4 collective-permute-start.10
  143.4 33.4 %collective-permute-start.11 = (bf16[512,768]{1,0:T(8,128)(2,1)S(1)}, bf16[512,768]{1,0:T(8,128)(2,1)S(1)}, u32[]{:S(2)}, u32[]{:S(2)}) collective-permute-start(bf16[512,768]{1,0:T(8,128)(2,1)S(1)} %convert_element_type.142), channel_id=1, source_target_pairs={{0,1},{1,0},{2,3},{3,2},{4,5},{5,4},{6,7},{7,6},{8,9},{9,8},{10,11... | collective-permute-start | bytes 2359304 | tf_op jit(solution)/shard_map/ppermute | solution.py:260
  143.6 6.1 %collective-permute-start.12 = (f32[6,768]{1,0:T(8,128)S(1)}, f32[6,768]{1,0:T(8,128)S(1)}, u32[]{:S(2)}, u32[]{:S(2)}) collective-permute-start(f32[6,768]{1,0:T(8,128)S(1)} %stack.93), channel_id=1, source_target_pairs={{0,1},{1,0},{2,3},{3,2},{4,5},{5,4},{6,7},{7,6},{8,9},{9,8},{10,11... | collective-permute-start | bytes 55304 | tf_op jit(solution)/shard_map/ppermute | solution.py:260
  148.0 45.7 %collective-permute-start.18 = (bf16[768,768]{1,0:T(8,128)(2,1)}, bf16[768,768]{1,0:T(8,128)(2,1)}, u32[]{:S(2)}, u32[]{:S(2)}) collective-permute-start(bf16[768,768]{1,0:T(8,128)(2,1)} %convolution_convert_fusion), channel_id=1, source_target_pairs={{0,2},{1,3},{2,0},{3,1},{4,6},{5,7},{6,4},{7,5},{8,10},{9,11},{10,... | collective-permute-start | bytes 3538952 | tf_op jit(solution)/shard_map/ppermute | solution.py:260
  149.7 27.0 %collective-permute-start.13 = (f32[7,768]{1,0:T(8,128)S(1)}, f32[7,768]{1,0:T(8,128)S(1)}, u32[]{:S(2)}, u32[]{:S(2)}) collective-permute-start(f32[7,768]{1,0:T(8,128)S(1)} %pad_maximum_fusion.11), channel_id=1, source_target_pairs={{0,2},{1,3},{2,0},{3,1},{4,6},{5,7},{6,4},{7,5},{8,10},{9,11},{10,... | collective-permute-start | bytes 64520 | tf_op jit(solution)/shard_map/ppermute | solution.py:260
  180.7 13.0 %copy-start.42 = (bf16[512,768]{1,0:T(8,128)(2,1)S(1)}, bf16[512,768]{1,0:T(8,128)(2,1)}, u32[]{:S(2)}) copy-start(bf16[512,768]{1,0:T(8,128)(2,1)} %copy-done.40) | copy-start | bytes 2359300
  198.0 44.8 %all-to-all-start.2 = ((bf16[8,112,768]{2,1,0:T(8,128)(2,1)}), bf16[8,112,768]{2,1,0:T(8,128)(2,1)S(1)}, u32[]{:S(2)}, u32[]{:S(2)}) async-start(bf16[8,112,768]{2,1,0:T(8,128)(2,1)} %pad_maximum_fusion.2), calls=%async_computation.2 | async-start | bytes 2752512 | tf_op jit(solution)/shard_map/all_to_all | solution.py:288
  208.5 25.0 %collective-permute-start.15 = (bf16[776,576]{1,0:T(8,128)(2,1)S(1)}, bf16[776,576]{1,0:T(8,128)(2,1)}, u32[]{:S(2)}, u32[]{:S(2)}) collective-permute-start(bf16[776,576]{1,0:T(8,128)(2,1)S(1)} %copy.57), channel_id=1, source_target_pairs={{0,2},{1,3},{2,0},{3,1},{4,6},{5,7},{6,4},{7,5},{8,10},{9,11},{10,... | collective-permute-start | bytes 2681864 | tf_op jit(solution)/shard_map/ppermute | solution.py:260
  214.4 44.4 %collective-permute-start.16 = (bf16[768,768]{1,0:T(8,128)(2,1)}, bf16[768,768]{1,0:T(8,128)(2,1)}, u32[]{:S(2)}, u32[]{:S(2)}) collective-permute-start(bf16[768,768]{1,0:T(8,128)(2,1)} %convolution_convert_fusion.1), channel_id=1, source_target_pairs={{0,2},{1,3},{2,0},{3,1},{4,6},{5,7},{6,4},{7,5},{8,10},{9,11},{10,... | collective-permute-start | bytes 3538952 | tf_op jit(solution)/shard_map/ppermute | solution.py:260
  242.9 8.5 %copy-start.4 = (bf16[8,112,768]{2,1,0:T(8,128)(2,1)}, bf16[8,112,768]{2,1,0:T(8,128)(2,1)S(1)}, u32[]{:S(2)}) copy-start(bf16[8,112,768]{2,1,0:T(8,128)(2,1)S(1)} %all-to-all-done.2) | copy-start | bytes 4128772
  242.9 28.6 %all-to-all-start = ((bf16[8,104,576]{2,1,0:T(8,128)(2,1)}), bf16[8,104,576]{2,1,0:T(8,128)(2,1)S(1)}, u32[]{:S(2)}, u32[]{:S(2)}) async-start(bf16[8,104,576]{2,1,0:T(8,128)(2,1)} %pad_maximum_fusion.3), calls=%async_computation | async-start | bytes 2129920 | tf_op jit(solution)/shard_map/all_to_all | solution.py:288
  251.3 11.8 %copy-start.10 = (bf16[1024,768]{1,0:T(8,128)(2,1)S(1)}, bf16[1024,768]{1,0:T(8,128)(2,1)}, u32[]{:S(2)}) copy-start(bf16[1024,768]{1,0:T(8,128)(2,1)} %fusion.17.upstream_ref) | copy-start | bytes 4718596
  251.3 11.8 %copy-start.45 = (bf16[1024,192]{1,0:T(8,128)(2,1)S(1)}, bf16[1024,192]{1,0:T(8,128)(2,1)}, u32[]{:S(2)}) copy-start(bf16[1024,192]{1,0:T(8,128)(2,1)} %get-tuple-element.35.context_ref) | copy-start | bytes 1179652
  251.3 11.8 %collective-permute-start.17 = (bf16[768,192]{0,1:T(8,128)(2,1)S(1)}, bf16[768,192]{0,1:T(8,128)(2,1)S(1)}, u32[]{:S(2)}, u32[]{:S(2)}) collective-permute-start(bf16[768,192]{0,1:T(8,128)(2,1)S(1)} %convolution_convert_fusion.4), channel_id=1, source_target_pairs={{0,2},{1,3},{2,0},{3,1},{4,6},{5,7},{6,4},{7,5},{8,10},{9,11},{10,... | collective-permute-start | bytes 884744 | tf_op jit(solution)/shard_map/ppermute | solution.py:260
  272.5 39.4 %all-to-all-start.1 = ((bf16[8,96,960]{2,1,0:T(8,128)(2,1)}), bf16[8,96,960]{2,1,0:T(8,128)(2,1)S(1)}, u32[]{:S(2)}, u32[]{:S(2)}) async-start(bf16[8,96,960]{2,1,0:T(8,128)(2,1)} %pad_maximum_fusion.1), calls=%async_computation.1 | async-start | bytes 3145728 | tf_op jit(solution)/shard_map/all_to_all | solution.py:288
  280.2 2.4 collective-permute-start.14
  286.4 27.3 %copy-start.1 = (bf16[768,768]{1,0:T(8,128)(2,1)S(1)}, bf16[768,768]{1,0:T(8,128)(2,1)}, u32[]{:S(2)}) copy-start(bf16[768,768]{1,0:T(8,128)(2,1)} %param.31) | copy-start | bytes 3538948
  (43 other events, 151.1 us)
